TPU v7x, 32 devices: a whole 2x2x4 slice. The times are simulated.
32 devices in a mesh: ens: 2 (over x), col: 4 (over z), row: 4 (over y, core).
Axes of the slice: x: 2, y: 2, z: 4, core: 2. Of those that a mesh axis runs over, the one named last changes fastest.
Arguments:
- u_init: float32 [8192, 4096], P(('ens', 'row'), 'col'), parts along dimension 0
- v_init: float32 [8192, 4096], P(('ens', 'row'), 'col'), parts along dimension 0
- stencil_w: float32 [48, 3, 3], replicated
Outputs:
- output 1: float32 [8192, 4096], P(('ens', 'row'), 'col'), parts along dimension 0
- output 2: float32 [8192, 4096], P(('ens', 'row'), 'col'), parts along dimension 0
There are 2 independent parts. A program takes and returns all parts, laid end to end along the dimension named above; an argument that names none is the same for every part.
All inputs are finite; a program needn't handle non-finite values.
Results may differ from a plain program's by a relative error of at most 0.001.
Values are sent between devices in bfloat16 or wider.
A program may use at most 1 GiB of HBM per device.

v0:
```python
import jax
import jax.numpy as jnp
from jax import lax
from jax.sharding import PartitionSpec as P

TIME_STEP = 0.5


def stencil_valid(block, step_w):
    out_rows = block.shape[0] - 2
    out_cols = block.shape[1] - 2
    total_acc = step_w[0, 0] * block[0:out_rows, 0:out_cols]
    for tap_index in range(1, 9):
        row_off, col_off = divmod(tap_index, 3)
        total_acc = total_acc + step_w[row_off, col_off] * block[row_off:row_off + out_rows, col_off:col_off + out_cols]
    return total_acc


def solution(mesh):
    row_devices = mesh.shape["row"]
    col_devices = mesh.shape["col"]
    row_fwd = [(source_dev, (source_dev + 1) % row_devices) for source_dev in range(row_devices)]
    row_back = [(source_dev, (source_dev - 1) % row_devices) for source_dev in range(row_devices)]
    col_fwd = [(source_dev, (source_dev + 1) % col_devices) for source_dev in range(col_devices)]
    col_back = [(source_dev, (source_dev - 1) % col_devices) for source_dev in range(col_devices)]
    tile_spec = P(("ens", "row"), "col")

    def halo_pad(u_tile):
        from_above = lax.ppermute(u_tile[-1:, :], "row", row_fwd)
        from_below = lax.ppermute(u_tile[:1, :], "row", row_back)
        tall_tile = jnp.concatenate([from_above, u_tile, from_below], axis=0)
        from_left = lax.ppermute(tall_tile[:, -1:], "col", col_fwd)
        from_right = lax.ppermute(tall_tile[:, :1], "col", col_back)
        return jnp.concatenate([from_left, tall_tile, from_right], axis=1)

    def local_run(u_tile, v_tile, stencil_w):
        def one_step(state_pair, step_w):
            u_now, v_now = state_pair
            padded = halo_pad(u_now)
            v_next = v_now + (stencil_valid(padded, step_w) - u_now)
            u_next = u_now + TIME_STEP * v_next
            return (u_next, v_next), None

        (u_final, v_final), _ = lax.scan(one_step, (u_tile, v_tile), stencil_w)
        return u_final, v_final

    return jax.shard_map(local_run, mesh=mesh, in_specs=(tile_spec, tile_spec, P()), out_specs=(tile_spec, tile_spec), check_vma=False)
```

profile of v0, /device:TPU:1, one launch (start us, length us, event | category | flops | bytes accessed | tf_op | source)
XLA Modules:
  0.0 2967.8 jit_solution(14077546045547573617)
XLA Ops:
  12.2 2944.8 %while.12 = (s32[]{:T(128)}, f32[1024,1024]{0,1:T(8,128)}, f32[1024,1024]{0,1:T(8,128)}, f32[48,3,3]{2,1,0:T(4,128)S(1)}, s32[]{:T(128)}) while((s32[]{:T(128)}, f32[1024,1024]{0,1:T(8,128)}, f32[1024,1024]{0,1:T(8,128)}, f32[48,3,3]{2,1,0:T(4,128)S(1)}, s32[]{:T(128)}) %tuple.44), condition=%wide.region_1.2_spmd, body=%wide.region_0.1_spmd.sunk | while | flops 30408704 | bytes 54665760 | solution.py:44
  46.6 32.0 %multiply_add_fusion.2 = (f32[1024,1024]{0,1:T(8,128)}, f32[1024,1024]{0,1:T(8,128)}) fusion(f32[1024,1024]{0,1:T(8,128)} %copy-done, f32[1024,1024]{0,1:T(8,128)} %get-tuple-element.122, f32[1026,1]{0,1:T(1,128)S(1)} %collective-permute-done.2, f32[1026,1024]{0,1:T(8,128)} %concatenate.21, f32[]{:T(128)} %bitcast.22, ...), kind=kLoop, calls=%fused_computation.34.clone.1 | loop fusion | flops 30408704 | bytes 20996148 | tf_op jit(solution)/shard_map/while/body/eval_jaxpr/add | solution.py:41
  109.3 32.0 %multiply_add_fusion.2 = (f32[1024,1024]{0,1:T(8,128)}, f32[1024,1024]{0,1:T(8,128)}) fusion(f32[1024,1024]{0,1:T(8,128)} %copy-done, f32[1024,1024]{0,1:T(8,128)} %get-tuple-element.122, f32[1026,1]{0,1:T(1,128)S(1)} %collective-permute-done.2, f32[1026,1024]{0,1:T(8,128)} %concatenate.21, f32[]{:T(128)} %bitcast.22, ...), kind=kLoop, calls=%fused_computation.34.clone.1 | loop fusion | flops 30408704 | bytes 20996148 | tf_op jit(solution)/shard_map/while/body/eval_jaxpr/add | solution.py:41
  171.9 32.0 %multiply_add_fusion.2 = (f32[1024,1024]{0,1:T(8,128)}, f32[1024,1024]{0,1:T(8,128)}) fusion(f32[1024,1024]{0,1:T(8,128)} %copy-done, f32[1024,1024]{0,1:T(8,128)} %get-tuple-element.122, f32[1026,1]{0,1:T(1,128)S(1)} %collective-permute-done.2, f32[1026,1024]{0,1:T(8,128)} %concatenate.21, f32[]{:T(128)} %bitcast.22, ...), kind=kLoop, calls=%fused_computation.34.clone.1 | loop fusion | flops 30408704 | bytes 20996148 | tf_op jit(solution)/shard_map/while/body/eval_jaxpr/add | solution.py:41
  234.7 32.0 %multiply_add_fusion.2 = (f32[1024,1024]{0,1:T(8,128)}, f32[1024,1024]{0,1:T(8,128)}) fusion(f32[1024,1024]{0,1:T(8,128)} %copy-done, f32[1024,1024]{0,1:T(8,128)} %get-tuple-element.122, f32[1026,1]{0,1:T(1,128)S(1)} %collective-permute-done.2, f32[1026,1024]{0,1:T(8,128)} %concatenate.21, f32[]{:T(128)} %bitcast.22, ...), kind=kLoop, calls=%fused_computation.34.clone.1 | loop fusion | flops 30408704 | bytes 20996148 | tf_op jit(solution)/shard_map/while/body/eval_jaxpr/add | solution.py:41
  297.7 32.0 %multiply_add_fusion.2 = (f32[1024,1024]{0,1:T(8,128)}, f32[1024,1024]{0,1:T(8,128)}) fusion(f32[1024,1024]{0,1:T(8,128)} %copy-done, f32[1024,1024]{0,1:T(8,128)} %get-tuple-element.122, f32[1026,1]{0,1:T(1,128)S(1)} %collective-permute-done.2, f32[1026,1024]{0,1:T(8,128)} %concatenate.21, f32[]{:T(128)} %bitcast.22, ...), kind=kLoop, calls=%fused_computation.34.clone.1 | loop fusion | flops 30408704 | bytes 20996148 | tf_op jit(solution)/shard_map/while/body/eval_jaxpr/add | solution.py:41
  361.1 32.0 %multiply_add_fusion.2 = (f32[1024,1024]{0,1:T(8,128)}, f32[1024,1024]{0,1:T(8,128)}) fusion(f32[1024,1024]{0,1:T(8,128)} %copy-done, f32[1024,1024]{0,1:T(8,128)} %get-tuple-element.122, f32[1026,1]{0,1:T(1,128)S(1)} %collective-permute-done.2, f32[1026,1024]{0,1:T(8,128)} %concatenate.21, f32[]{:T(128)} %bitcast.22, ...), kind=kLoop, calls=%fused_computation.34.clone.1 | loop fusion | flops 30408704 | bytes 20996148 | tf_op jit(solution)/shard_map/while/body/eval_jaxpr/add | solution.py:41
  424.2 32.0 %multiply_add_fusion.2 = (f32[1024,1024]{0,1:T(8,128)}, f32[1024,1024]{0,1:T(8,128)}) fusion(f32[1024,1024]{0,1:T(8,128)} %copy-done, f32[1024,1024]{0,1:T(8,128)} %get-tuple-element.122, f32[1026,1]{0,1:T(1,128)S(1)} %collective-permute-done.2, f32[1026,1024]{0,1:T(8,128)} %concatenate.21, f32[]{:T(128)} %bitcast.22, ...), kind=kLoop, calls=%fused_computation.34.clone.1 | loop fusion | flops 30408704 | bytes 20996148 | tf_op jit(solution)/shard_map/while/body/eval_jaxpr/add | solution.py:41
  487.1 32.0 %multiply_add_fusion.2 = (f32[1024,1024]{0,1:T(8,128)}, f32[1024,1024]{0,1:T(8,128)}) fusion(f32[1024,1024]{0,1:T(8,128)} %copy-done, f32[1024,1024]{0,1:T(8,128)} %get-tuple-element.122, f32[1026,1]{0,1:T(1,128)S(1)} %collective-permute-done.2, f32[1026,1024]{0,1:T(8,128)} %concatenate.21, f32[]{:T(128)} %bitcast.22, ...), kind=kLoop, calls=%fused_computation.34.clone.1 | loop fusion | flops 30408704 | bytes 20996148 | tf_op jit(solution)/shard_map/while/body/eval_jaxpr/add | solution.py:41
  549.9 32.0 %multiply_add_fusion.2 = (f32[1024,1024]{0,1:T(8,128)}, f32[1024,1024]{0,1:T(8,128)}) fusion(f32[1024,1024]{0,1:T(8,128)} %copy-done, f32[1024,1024]{0,1:T(8,128)} %get-tuple-element.122, f32[1026,1]{0,1:T(1,128)S(1)} %collective-permute-done.2, f32[1026,1024]{0,1:T(8,128)} %concatenate.21, f32[]{:T(128)} %bitcast.22, ...), kind=kLoop, calls=%fused_computation.34.clone.1 | loop fusion | flops 30408704 | bytes 20996148 | tf_op jit(solution)/shard_map/while/body/eval_jaxpr/add | solution.py:41
  612.7 32.0 %multiply_add_fusion.2 = (f32[1024,1024]{0,1:T(8,128)}, f32[1024,1024]{0,1:T(8,128)}) fusion(f32[1024,1024]{0,1:T(8,128)} %copy-done, f32[1024,1024]{0,1:T(8,128)} %get-tuple-element.122, f32[1026,1]{0,1:T(1,128)S(1)} %collective-permute-done.2, f32[1026,1024]{0,1:T(8,128)} %concatenate.21, f32[]{:T(128)} %bitcast.22, ...), kind=kLoop, calls=%fused_computation.34.clone.1 | loop fusion | flops 30408704 | bytes 20996148 | tf_op jit(solution)/shard_map/while/body/eval_jaxpr/add | solution.py:41
  675.0 32.0 %multiply_add_fusion.2 = (f32[1024,1024]{0,1:T(8,128)}, f32[1024,1024]{0,1:T(8,128)}) fusion(f32[1024,1024]{0,1:T(8,128)} %copy-done, f32[1024,1024]{0,1:T(8,128)} %get-tuple-element.122, f32[1026,1]{0,1:T(1,128)S(1)} %collective-permute-done.2, f32[1026,1024]{0,1:T(8,128)} %concatenate.21, f32[]{:T(128)} %bitcast.22, ...), kind=kLoop, calls=%fused_computation.34.clone.1 | loop fusion | flops 30408704 | bytes 20996148 | tf_op jit(solution)/shard_map/while/body/eval_jaxpr/add | solution.py:41
  737.1 32.0 %multiply_add_fusion.2 = (f32[1024,1024]{0,1:T(8,128)}, f32[1024,1024]{0,1:T(8,128)}) fusion(f32[1024,1024]{0,1:T(8,128)} %copy-done, f32[1024,1024]{0,1:T(8,128)} %get-tuple-element.122, f32[1026,1]{0,1:T(1,128)S(1)} %collective-permute-done.2, f32[1026,1024]{0,1:T(8,128)} %concatenate.21, f32[]{:T(128)} %bitcast.22, ...), kind=kLoop, calls=%fused_computation.34.clone.1 | loop fusion | flops 30408704 | bytes 20996148 | tf_op jit(solution)/shard_map/while/body/eval_jaxpr/add | solution.py:41
  799.1 32.0 %multiply_add_fusion.2 = (f32[1024,1024]{0,1:T(8,128)}, f32[1024,1024]{0,1:T(8,128)}) fusion(f32[1024,1024]{0,1:T(8,128)} %copy-done, f32[1024,1024]{0,1:T(8,128)} %get-tuple-element.122, f32[1026,1]{0,1:T(1,128)S(1)} %collective-permute-done.2, f32[1026,1024]{0,1:T(8,128)} %concatenate.21, f32[]{:T(128)} %bitcast.22, ...), kind=kLoop, calls=%fused_computation.34.clone.1 | loop fusion | flops 30408704 | bytes 20996148 | tf_op jit(solution)/shard_map/while/body/eval_jaxpr/add | solution.py:41
  861.0 32.0 %multiply_add_fusion.2 = (f32[1024,1024]{0,1:T(8,128)}, f32[1024,1024]{0,1:T(8,128)}) fusion(f32[1024,1024]{0,1:T(8,128)} %copy-done, f32[1024,1024]{0,1:T(8,128)} %get-tuple-element.122, f32[1026,1]{0,1:T(1,128)S(1)} %collective-permute-done.2, f32[1026,1024]{0,1:T(8,128)} %concatenate.21, f32[]{:T(128)} %bitcast.22, ...), kind=kLoop, calls=%fused_computation.34.clone.1 | loop fusion | flops 30408704 | bytes 20996148 | tf_op jit(solution)/shard_map/while/body/eval_jaxpr/add | solution.py:41
  922.6 32.0 %multiply_add_fusion.2 = (f32[1024,1024]{0,1:T(8,128)}, f32[1024,1024]{0,1:T(8,128)}) fusion(f32[1024,1024]{0,1:T(8,128)} %copy-done, f32[1024,1024]{0,1:T(8,128)} %get-tuple-element.122, f32[1026,1]{0,1:T(1,128)S(1)} %collective-permute-done.2, f32[1026,1024]{0,1:T(8,128)} %concatenate.21, f32[]{:T(128)} %bitcast.22, ...), kind=kLoop, calls=%fused_computation.34.clone.1 | loop fusion | flops 30408704 | bytes 20996148 | tf_op jit(solution)/shard_map/while/body/eval_jaxpr/add | solution.py:41
  984.1 32.0 %multiply_add_fusion.2 = (f32[1024,1024]{0,1:T(8,128)}, f32[1024,1024]{0,1:T(8,128)}) fusion(f32[1024,1024]{0,1:T(8,128)} %copy-done, f32[1024,1024]{0,1:T(8,128)} %get-tuple-element.122, f32[1026,1]{0,1:T(1,128)S(1)} %collective-permute-done.2, f32[1026,1024]{0,1:T(8,128)} %concatenate.21, f32[]{:T(128)} %bitcast.22, ...), kind=kLoop, calls=%fused_computation.34.clone.1 | loop fusion | flops 30408704 | bytes 20996148 | tf_op jit(solution)/shard_map/while/body/eval_jaxpr/add | solution.py:41
  1045.4 32.0 %multiply_add_fusion.2 = (f32[1024,1024]{0,1:T(8,128)}, f32[1024,1024]{0,1:T(8,128)}) fusion(f32[1024,1024]{0,1:T(8,128)} %copy-done, f32[1024,1024]{0,1:T(8,128)} %get-tuple-element.122, f32[1026,1]{0,1:T(1,128)S(1)} %collective-permute-done.2, f32[1026,1024]{0,1:T(8,128)} %concatenate.21, f32[]{:T(128)} %bitcast.22, ...), kind=kLoop, calls=%fused_computation.34.clone.1 | loop fusion | flops 30408704 | bytes 20996148 | tf_op jit(solution)/shard_map/while/body/eval_jaxpr/add | solution.py:41
  1106.5 32.0 %multiply_add_fusion.2 = (f32[1024,1024]{0,1:T(8,128)}, f32[1024,1024]{0,1:T(8,128)}) fusion(f32[1024,1024]{0,1:T(8,128)} %copy-done, f32[1024,1024]{0,1:T(8,128)} %get-tuple-element.122, f32[1026,1]{0,1:T(1,128)S(1)} %collective-permute-done.2, f32[1026,1024]{0,1:T(8,128)} %concatenate.21, f32[]{:T(128)} %bitcast.22, ...), kind=kLoop, calls=%fused_computation.34.clone.1 | loop fusion | flops 30408704 | bytes 20996148 | tf_op jit(solution)/shard_map/while/body/eval_jaxpr/add | solution.py:41
  1167.4 32.0 %multiply_add_fusion.2 = (f32[1024,1024]{0,1:T(8,128)}, f32[1024,1024]{0,1:T(8,128)}) fusion(f32[1024,1024]{0,1:T(8,128)} %copy-done, f32[1024,1024]{0,1:T(8,128)} %get-tuple-element.122, f32[1026,1]{0,1:T(1,128)S(1)} %collective-permute-done.2, f32[1026,1024]{0,1:T(8,128)} %concatenate.21, f32[]{:T(128)} %bitcast.22, ...), kind=kLoop, calls=%fused_computation.34.clone.1 | loop fusion | flops 30408704 | bytes 20996148 | tf_op jit(solution)/shard_map/while/body/eval_jaxpr/add | solution.py:41
  1228.2 32.0 %multiply_add_fusion.2 = (f32[1024,1024]{0,1:T(8,128)}, f32[1024,1024]{0,1:T(8,128)}) fusion(f32[1024,1024]{0,1:T(8,128)} %copy-done, f32[1024,1024]{0,1:T(8,128)} %get-tuple-element.122, f32[1026,1]{0,1:T(1,128)S(1)} %collective-permute-done.2, f32[1026,1024]{0,1:T(8,128)} %concatenate.21, f32[]{:T(128)} %bitcast.22, ...), kind=kLoop, calls=%fused_computation.34.clone.1 | loop fusion | flops 30408704 | bytes 20996148 | tf_op jit(solution)/shard_map/while/body/eval_jaxpr/add | solution.py:41
  2440.2 32.0 %multiply_add_fusion.2 = (f32[1024,1024]{0,1:T(8,128)}, f32[1024,1024]{0,1:T(8,128)}) fusion(f32[1024,1024]{0,1:T(8,128)} %copy-done, f32[1024,1024]{0,1:T(8,128)} %get-tuple-element.122, f32[1026,1]{0,1:T(1,128)S(1)} %collective-permute-done.2, f32[1026,1024]{0,1:T(8,128)} %concatenate.21, f32[]{:T(128)} %bitcast.22, ...), kind=kLoop, calls=%fused_computation.34.clone.1 | loop fusion | flops 30408704 | bytes 20996148 | tf_op jit(solution)/shard_map/while/body/eval_jaxpr/add | solution.py:41
  2561.4 32.0 %multiply_add_fusion.2 = (f32[1024,1024]{0,1:T(8,128)}, f32[1024,1024]{0,1:T(8,128)}) fusion(f32[1024,1024]{0,1:T(8,128)} %copy-done, f32[1024,1024]{0,1:T(8,128)} %get-tuple-element.122, f32[1026,1]{0,1:T(1,128)S(1)} %collective-permute-done.2, f32[1026,1024]{0,1:T(8,128)} %concatenate.21, f32[]{:T(128)} %bitcast.22, ...), kind=kLoop, calls=%fused_computation.34.clone.1 | loop fusion | flops 30408704 | bytes 20996148 | tf_op jit(solution)/shard_map/while/body/eval_jaxpr/add | solution.py:41
  2682.6 32.0 %multiply_add_fusion.2 = (f32[1024,1024]{0,1:T(8,128)}, f32[1024,1024]{0,1:T(8,128)}) fusion(f32[1024,1024]{0,1:T(8,128)} %copy-done, f32[1024,1024]{0,1:T(8,128)} %get-tuple-element.122, f32[1026,1]{0,1:T(1,128)S(1)} %collective-permute-done.2, f32[1026,1024]{0,1:T(8,128)} %concatenate.21, f32[]{:T(128)} %bitcast.22, ...), kind=kLoop, calls=%fused_computation.34.clone.1 | loop fusion | flops 30408704 | bytes 20996148 | tf_op jit(solution)/shard_map/while/body/eval_jaxpr/add | solution.py:41
  (798 shorter events, 2229.5 us)
Async XLA Ops:
  16.6 14.3 collective-permute-start
  83.0 13.6 collective-permute-start
  145.7 13.9 collective-permute-start
  208.4 14.4 collective-permute-start
  271.2 15.0 collective-permute-start
  334.2 15.3 collective-permute-start
  397.5 15.1 collective-permute-start
  460.6 14.9 collective-permute-start
  523.6 14.7 collective-permute-start
  586.3 14.6 collective-permute-start
  649.2 14.1 collective-permute-start
  711.4 14.1 collective-permute-start
  773.5 14.0 collective-permute-start
  835.5 13.8 collective-permute-start
  897.4 13.7 collective-permute-start
  959.1 13.5 collective-permute-start
  1020.5 13.3 collective-permute-start
  1081.8 13.1 collective-permute-start
  1142.9 12.9 collective-permute-start
  1203.9 12.7 collective-permute-start
  1688.7 12.7 collective-permute-start
  1809.9 12.7 collective-permute-start
  1931.1 12.7 collective-permute-start
  2052.3 12.7 collective-permute-start
  (216 other events, 1197.6 us)
where the time goes:
time: 2980 us; the launch traced here: 2970 us
  other arithmetic  1540 us (52%)
  local copies, waits for them, and re-layouts  612 us (21%)
  waiting for transfers between devices  567 us (19%)
  starting transfers between devices  250 us (8%)
    add x48, other arithmetic, one_step(): u_next = u_now + TIME_STEP * v_next  1540 us
    ppermute x48, waiting for transfers between devices, halo_pad(): from_above = lax.ppermute(u_tile[-1:, :], 'row', row_fwd)  458 us
    concatenate x48, local copies, waits for them, and re-layouts, halo_pad(): tall_tile = jnp.concatenate([from_above, u_tile, from_below], axis=0)  307 us
    while x144, local copies, waits for them, and re-layouts  202 us
    ppermute x48, starting transfers between devices, halo_pad(): from_above = lax.ppermute(u_tile[-1:, :], 'row', row_fwd)  175 us
    ppermute x48, waiting for transfers between devices, halo_pad(): from_left = lax.ppermute(tall_tile[:, -1:], 'col', col_fwd)  83.5 us
    ppermute x48, starting transfers between devices, halo_pad(): from_left = lax.ppermute(tall_tile[:, -1:], 'col', col_fwd)  68.3 us
  transfers between devices with their start and end apart: 192, of which 147 were waited for; matrix products, arithmetic and copies ran while one was open for 1% of the time, Pallas kernels for 0%

commit v1 on v0

v1 whole, which is shorter than its diff:
```python
import functools

import jax
import jax.numpy as jnp
from jax import lax
from jax.experimental import pallas as pl
from jax.experimental.pallas import tpu as pltpu
from jax.sharding import PartitionSpec as P

LANES = 128
PLANES = 9
HALO = 64
STAGE = 16


def step_weights(w_ref, t):
    return (
        1.5 + 0.5 * w_ref[1, 1, t],
        0.5 * w_ref[0, 0, t],
        0.5 * w_ref[0, 1, t],
        0.5 * w_ref[0, 2, t],
        0.5 * w_ref[1, 0, t],
    )


def chunk(now, old, weights, start, groups):
    centre, w00, w01, w02, w10 = weights

    def taps(g, p):
        return [now[p, pl.ds(start + (8 * g + d), 8), :] for d in (-1, 0, 1)]

    def update(g, p, up, mid, down):
        cols = pl.ds(start + 8 * g, 8)
        new = (
            (centre * mid[1] - old[p, cols, :])
            + w01 * (up[1] + down[1])
            + w10 * (mid[0] + mid[2])
            + w00 * (up[0] + down[2])
            + w02 * (up[2] + down[0])
        )
        old[p, cols, :] = new
        return new

    ghosts = []
    for g in range(groups):
        last = update(g, PLANES, taps(g, PLANES - 1), taps(g, PLANES), taps(g, PLANES + 1))
        first = update(g, 1, taps(g, 0), taps(g, 1), taps(g, 2))
        ghosts.append((pltpu.roll(last, 1, 1), pltpu.roll(first, LANES - 1, 1)))
    for g in range(groups):
        up, mid = taps(g, 1), taps(g, 2)
        for p in range(2, PLANES):
            down = taps(g, p + 1)
            update(g, p, up, mid, down)
            up, mid = mid, down
    for g in range(groups):
        cols = pl.ds(start + 8 * g, 8)
        old[0, cols, :] = ghosts[g][0]
        old[PLANES + 1, cols, :] = ghosts[g][1]


def sweep(now, old, weights, first_col, width):
    first = first_col + HALO
    done = 0
    for groups in (2,):
        cols = 8 * groups
        count = (width - done) // cols
        base = first + done

        def body(i, carry, groups=groups, cols=cols, base=base):
            chunk(now, old, weights, pl.multiple_of(base + i * cols, 8), groups)
            return carry

        lax.fori_loop(0, count, body, 0)
        done = done + count * cols


def kernel(n_row, n_col, steps, u_hbm, v_hbm, w_ref, uo_hbm, vo_hbm, even, odd, u_nat, v_nat, load_sem, store_sem,
           row_send, row_recv, col_send, col_recv):
    rows, cols = u_hbm.shape
    blocks = cols // LANES
    row_id, col_id = lax.axis_index("row"), lax.axis_index("col")
    above, below = lax.rem(row_id + n_row - 1, n_row), lax.rem(row_id + 1, n_row)
    left, right = lax.rem(col_id + n_col - 1, n_col), lax.rem(col_id + 1, n_col)

    def load(f, q):
        src, dst = ((u_hbm, u_nat), (v_hbm, v_nat))[f]
        return pltpu.make_async_copy(
            src.at[:, pl.ds(q * LANES, LANES)], dst.at[q, pl.ds(HALO, rows), :], load_sem.at[f, q])

    def row_copy(f, side, q):
        src, dst = ((u_hbm, u_nat), (v_hbm, v_nat))[f]
        depth = steps
        lines = (rows - depth, 0)[side]
        place = (HALO - depth, HALO + rows)[side]
        return pltpu.make_async_remote_copy(
            src_ref=src.at[pl.ds(lines, depth), pl.ds(q * LANES, LANES)],
            dst_ref=dst.at[q, pl.ds(place, depth), :],
            send_sem=row_send.at[f, side, q], recv_sem=row_recv.at[f, side, q],
            device_id={"row": (below, above)[side]}, device_id_type=pl.DeviceIdType.MESH)

    def col_copy(f, side):
        ref = (even, odd)[f]
        depth = steps
        lines = (HALO + cols - depth, HALO)[side]
        place = (HALO - depth, HALO + cols)[side]
        return pltpu.make_async_remote_copy(
            src_ref=ref.at[:, pl.ds(lines, depth), :], dst_ref=ref.at[:, pl.ds(place, depth), :],
            send_sem=col_send.at[f, side], recv_sem=col_recv.at[f, side],
            device_id={"col": (right, left)[side]}, device_id_type=pl.DeviceIdType.MESH)

    order = [0, blocks - 1] + list(range(1, blocks - 1))
    for q in order:
        for f in (0, 1):
            load(f, q).start()

    barrier = pltpu.get_barrier_semaphore()
    for peer in ({"row": above}, {"row": below}, {"col": left}, {"col": right}):
        pl.semaphore_signal(barrier, inc=1, device_id=peer, device_id_type=pl.DeviceIdType.MESH)
    pl.semaphore_wait(barrier, 4)

    for q in order:
        for f in (0, 1):
            for side in (0, 1):
                row_copy(f, side, q).start()

    for q in order:
        for f in (0, 1):
            load(f, q).wait()
            for side in (0, 1):
                row_copy(f, side, q).wait()

        for s in range(PLANES):
            lines = pl.ds(s, LANES, stride=PLANES)
            u_now = 0.25 * u_nat[q, lines, :]
            u_old = u_now - 0.125 * v_nat[q, lines, :]
            words = pl.ds(HALO + q * LANES, LANES)
            u_now = jnp.transpose(u_now)
            even[s + 1, words, :] = u_now
            odd[s + 1, words, :] = jnp.transpose(u_old)
            if s == 0:
                even[PLANES + 1, words, :] = pltpu.roll(u_now, LANES - 1, 1)
            if s == PLANES - 1:
                even[0, words, :] = pltpu.roll(u_now, 1, 1)

    for f in (0, 1):
        for side in (0, 1):
            col_copy(f, side).start()

    pairs = max(1, min(14, (cols - 160) // 64) // 2)

    def inner_first(t):
        return HALO + STAGE * t

    def outer_first(t):
        return -STAGE * ((steps - 1 - t + STAGE - 1) // STAGE)

    def both(first_pair, last_pair, ranges):
        def body(tt, carry):
            for odd_step, (now, old) in enumerate(((even, odd), (odd, even))):
                t = 2 * tt + odd_step
                ranges(now, old, step_weights(w_ref, t), t)
            return carry

        lax.fori_loop(first_pair, last_pair, body, 0)

    def inner(now, old, weights, t):
        first = inner_first(t)
        sweep(now, old, weights, first, cols - 2 * first)

    def edges(now, old, weights, t):
        first, width = outer_first(t), inner_first(t) - outer_first(t)

        def side(i, carry):
            sweep(now, old, weights, first + i * (cols - first - width - first), width)
            return carry

        lax.fori_loop(0, 2, side, 0)

    def full(now, old, weights, t):
        first = outer_first(t)
        sweep(now, old, weights, first, cols - 2 * first)

    both(0, pairs, inner)
    for f in (0, 1):
        for side in (0, 1):
            col_copy(f, side).wait()
    both(0, pairs, edges)
    both(pairs, steps // 2, full)

    def store(f, q):
        src, dst = ((u_nat, uo_hbm), (v_nat, vo_hbm))[f]
        return pltpu.make_async_copy(
            src.at[q, pl.ds(HALO, rows), :], dst.at[:, pl.ds(q * LANES, LANES)], store_sem.at[f, q])

    for q in range(blocks):
        words = pl.ds(HALO + q * LANES, LANES)
        for s in range(PLANES):
            lines = pl.ds(s, LANES, stride=PLANES)
            u_now = even[s + 1, words, :]
            u_nat[q, lines, :] = jnp.transpose(4.0 * u_now)
            v_nat[q, lines, :] = jnp.transpose(8.0 * (u_now - odd[s + 1, words, :]))
        for f in (0, 1):
            store(f, q).start()
    for q in range(blocks):
        for f in (0, 1):
            store(f, q).wait()


def solution(mesh):
    n_row, n_col = mesh.shape["row"], mesh.shape["col"]
    tile_spec = P(("ens", "row"), "col")

    def local_run(u_tile, v_tile, stencil_w):
        rows, cols = u_tile.shape
        steps = stencil_w.shape[0]
        blocks = cols // LANES
        assert rows + 2 * HALO == LANES * PLANES and steps % 2 == 0 and steps < HALO
        native = pltpu.VMEM((blocks, rows + 2 * HALO, LANES), jnp.float32)
        level = pltpu.VMEM((PLANES + 2, cols + 2 * HALO, LANES), jnp.float32)
        hbm = pl.BlockSpec(memory_space=pl.ANY)
        tile = jax.ShapeDtypeStruct((rows, cols), jnp.float32)
        dma = pltpu.SemaphoreType.DMA
        return pl.pallas_call(
            functools.partial(kernel, n_row, n_col, steps),
            out_shape=(tile, tile),
            in_specs=[hbm, hbm, pl.BlockSpec(memory_space=pltpu.SMEM)],
            out_specs=(hbm, hbm),
            scratch_shapes=[
                level, level, native, native,
                dma((2, blocks)), dma((2, blocks)),
                dma((2, 2, blocks)), dma((2, 2, blocks)), dma((2, 2)), dma((2, 2)),
            ],
            compiler_params=pltpu.CompilerParams(
                collective_id=0, has_side_effects=True, vmem_limit_bytes=56 * 2**20),
            name="wave",
        )(u_tile, v_tile, jnp.transpose(stencil_w, (1, 2, 0)))

    return jax.shard_map(
        local_run, mesh=mesh, in_specs=(tile_spec, tile_spec, P()), out_specs=(tile_spec, tile_spec), check_vma=False)
```

time: 2980 us -> 385 us (0.13)
  other arithmetic: 1540 us -> 0 us
  local copies, waits for them, and re-layouts: 612 us -> 6.96 us
  waiting for transfers between devices: 567 us -> 0 us
  Pallas kernels: 0 us -> 377 us
  starting transfers between devices: 250 us -> 0 us
    add x48 -> x0, other arithmetic: 1540 us -> none  [one_step(): u_next = u_now + TIME_STEP * v_next]
    ppermute x192 -> x0, waiting for transfers between devices: 567 us -> none  [the longest x48 458 us: halo_pad(): from_above = lax.ppermute(u_tile[-1:, :], 'row', row_fwd)]
    pallas_call x0 -> x1, Pallas kernels: none -> 377 us  [local_run(): pl.pallas_call(functools.partial(kernel, n_row, n_col, steps), out_shape=...]
    concatenate x48 -> x0, local copies, waits for them, and re-layouts: 307 us -> none  [halo_pad(): tall_tile = jnp.concatenate([from_above, u_tile, from_below], axis=0)]
    ppermute x192 -> x0, starting transfers between devices: 250 us -> none  [the longest x48 175 us: halo_pad(): from_above = lax.ppermute(u_tile[-1:, :], 'row', row_fwd)]
    while x147 -> x0, local copies, waits for them, and re-layouts: 213 us -> none
    slice x144 -> x0, local copies, waits for them, and re-layouts: 80.6 us -> none  [the longest x48 38.1 us: halo_pad(): from_left = lax.ppermute(tall_tile[:, -1:], 'col', col_fwd)]
  transfers between devices with their start and end apart: 192 -> 0, of which waited for: 147 -> 0; matrix products, arithmetic and copies ran while one was open for 1% -> 0% of each run, Pallas kernels for 0% -> 0%
where the time goes in v1:
time: 385 us
  Pallas kernels  377 us (98%)
  local copies, waits for them, and re-layouts  6.96 us (2%)
    pallas_call x1, Pallas kernels, local_run(): pl.pallas_call(functools.partial(kernel, n_row, n_col, steps), out_shape=...  377 us

profile of v1, /device:TPU:1, one launch (start us, length us, event | category | flops | bytes accessed | tf_op | source)
XLA Modules:
  0.0 385.0 jit_solution(6005795906572596874)
XLA Ops:
  0.6 377.4 %wave.1 = (f32[1024,1024]{1,0:T(8,128)}, f32[1024,1024]{1,0:T(8,128)}) custom-call(f32[1024,1024]{1,0:T(8,128)} %u_hbm.1, f32[1024,1024]{1,0:T(8,128)} %v_hbm.1, f32[3,3,48]{2,1,0:T(4,128)} %bitcast.1), custom_call_target="tpu_custom_call" | custom-call | tf_op jit(solution)/shard_map/wave/pallas_call | solution.py:223
  378.1 0.0 copy-start
  378.1 4.9 %copy.7 = f32[1024,1024]{1,0:T(8,128)} copy(f32[1024,1024]{1,0:T(8,128)} %get-tuple-element.4) | data formatting | bytes 8388608
  383.0 0.0 copy-done
  383.0 2.0 copy.8
Async XLA Ops:
  378.1 5.0 %copy-start = (f32[1024,1024]{1,0:T(8,128)S(1)}, f32[1024,1024]{1,0:T(8,128)}, u32[]{:S(2)}) copy-start(f32[1024,1024]{1,0:T(8,128)} %get-tuple-element.5) | copy-start | bytes 12582916

commit v2 on v1

--- a/solution.py
+++ b/solution.py
@@ -10,7 +10,11 @@
 LANES = 128
 PLANES = 9
 HALO = 64
+MARGIN = 128
+INNER = 96
 STAGE = 16
+WIDE = 32
+BLOCKS = 4
 
 
 def step_weights(w_ref, t):
@@ -23,14 +27,14 @@
     )
 
 
-def chunk(now, old, weights, start, groups):
+def chunk(now, old, weights, start, blocks, own_ghosts):
     centre, w00, w01, w02, w10 = weights
 
-    def taps(g, p):
-        return [now[p, pl.ds(start + (8 * g + d), 8), :] for d in (-1, 0, 1)]
-
-    def update(g, p, up, mid, down):
-        cols = pl.ds(start + 8 * g, 8)
+    def taps(b, p):
+        return [now[p, pl.ds(start + (WIDE * b + d), WIDE), :] for d in (-1, 0, 1)]
+
+    def update(b, p, up, mid, down):
+        cols = pl.ds(start + WIDE * b, WIDE)
         new = (
             (centre * mid[1] - old[p, cols, :])
             + w01 * (up[1] + down[1])
@@ -41,37 +45,40 @@
         old[p, cols, :] = new
         return new
 
-    ghosts = []
-    for g in range(groups):
-        last = update(g, PLANES, taps(g, PLANES - 1), taps(g, PLANES), taps(g, PLANES + 1))
-        first = update(g, 1, taps(g, 0), taps(g, 1), taps(g, 2))
-        ghosts.append((pltpu.roll(last, 1, 1), pltpu.roll(first, LANES - 1, 1)))
-    for g in range(groups):
-        up, mid = taps(g, 1), taps(g, 2)
+    cols = pl.ds(start - WIDE, WIDE)
+    ghosts = [(cols, pltpu.roll(old[PLANES, cols, :], 1, 1), pltpu.roll(old[1, cols, :], LANES - 1, 1))]
+    for b in range(blocks):
+        cols = pl.ds(start + WIDE * b, WIDE)
+        last = update(b, PLANES, taps(b, PLANES - 1), taps(b, PLANES), taps(b, PLANES + 1))
+        first = update(b, 1, taps(b, 0), taps(b, 1), taps(b, 2))
+        if own_ghosts:
+            ghosts.append((cols, pltpu.roll(last, 1, 1), pltpu.roll(first, LANES - 1, 1)))
+    for b in range(blocks):
+        up, mid = taps(b, 1), taps(b, 2)
         for p in range(2, PLANES):
-            down = taps(g, p + 1)
-            update(g, p, up, mid, down)
+            down = taps(b, p + 1)
+            update(b, p, up, mid, down)
             up, mid = mid, down
-    for g in range(groups):
-        cols = pl.ds(start + 8 * g, 8)
-        old[0, cols, :] = ghosts[g][0]
-        old[PLANES + 1, cols, :] = ghosts[g][1]
+    for cols, top, bottom in ghosts:
+        old[0, cols, :] = top
+        old[PLANES + 1, cols, :] = bottom
 
 
 def sweep(now, old, weights, first_col, width):
-    first = first_col + HALO
-    done = 0
-    for groups in (2,):
-        cols = 8 * groups
-        count = (width - done) // cols
-        base = first + done
-
-        def body(i, carry, groups=groups, cols=cols, base=base):
-            chunk(now, old, weights, pl.multiple_of(base + i * cols, 8), groups)
-            return carry
-
-        lax.fori_loop(0, count, body, 0)
-        done = done + count * cols
+    first = first_col + MARGIN
+    small, large = WIDE, WIDE * BLOCKS
+    few = lax.div(lax.rem(width, large), small)
+
+    def remainder(i, carry):
+        chunk(now, old, weights, pl.multiple_of(first + i * small, 8), 1, False)
+        return carry
+
+    def body(i, carry):
+        chunk(now, old, weights, pl.multiple_of(first + few * small + i * large, 8), BLOCKS, True)
+        return carry
+
+    lax.fori_loop(0, few, remainder, 0)
+    lax.fori_loop(0, lax.div(width, large), body, 0)
 
 
 def kernel(n_row, n_col, steps, u_hbm, v_hbm, w_ref, uo_hbm, vo_hbm, even, odd, u_nat, v_nat, load_sem, store_sem,
@@ -99,12 +106,12 @@
             device_id={"row": (below, above)[side]}, device_id_type=pl.DeviceIdType.MESH)
 
     def col_copy(f, side):
-        ref = (even, odd)[f]
+        ref, planes = ((even, pl.ds(0, PLANES + 2)), (odd, pl.ds(1, PLANES)))[f]
         depth = steps
-        lines = (HALO + cols - depth, HALO)[side]
-        place = (HALO - depth, HALO + cols)[side]
+        lines = (MARGIN + cols - depth, MARGIN)[side]
+        place = (MARGIN - depth, MARGIN + cols)[side]
         return pltpu.make_async_remote_copy(
-            src_ref=ref.at[:, pl.ds(lines, depth), :], dst_ref=ref.at[:, pl.ds(place, depth), :],
+            src_ref=ref.at[planes, pl.ds(lines, depth), :], dst_ref=ref.at[planes, pl.ds(place, depth), :],
             send_sem=col_send.at[f, side], recv_sem=col_recv.at[f, side],
             device_id={"col": (right, left)[side]}, device_id_type=pl.DeviceIdType.MESH)
 
@@ -123,7 +130,11 @@
             for side in (0, 1):
                 row_copy(f, side, q).start()
 
-    for q in order:
+    for place, q in enumerate(order):
+        if place == 3:
+            for f in (0, 1):
+                for side in (0, 1):
+                    col_copy(f, side).start()
         for f in (0, 1):
             load(f, q).wait()
             for side in (0, 1):
@@ -133,7 +144,7 @@
             lines = pl.ds(s, LANES, stride=PLANES)
             u_now = 0.25 * u_nat[q, lines, :]
             u_old = u_now - 0.125 * v_nat[q, lines, :]
-            words = pl.ds(HALO + q * LANES, LANES)
+            words = pl.ds(MARGIN + q * LANES, LANES)
             u_now = jnp.transpose(u_now)
             even[s + 1, words, :] = u_now
             odd[s + 1, words, :] = jnp.transpose(u_old)
@@ -142,50 +153,43 @@
             if s == PLANES - 1:
                 even[0, words, :] = pltpu.roll(u_now, 1, 1)
 
-    for f in (0, 1):
-        for side in (0, 1):
-            col_copy(f, side).start()
-
-    pairs = max(1, min(14, (cols - 160) // 64) // 2)
-
-    def inner_first(t):
-        return HALO + STAGE * t
-
-    def outer_first(t):
-        return -STAGE * ((steps - 1 - t + STAGE - 1) // STAGE)
-
-    def both(first_pair, last_pair, ranges):
-        def body(tt, carry):
+    pairs = min(14, (cols - 2 * INNER - 32) // (2 * STAGE)) // 2
+
+    def advance(begin_pair, end_pair, sides, span):
+        def pair(v, carry):
             for odd_step, (now, old) in enumerate(((even, odd), (odd, even))):
-                t = 2 * tt + odd_step
-                ranges(now, old, step_weights(w_ref, t), t)
+                t = 2 * v + odd_step
+                weights = step_weights(w_ref, t)
+                first, width, shift = span(t)
+
+                def side(i, carry, now=now, old=old, first=first, width=width, shift=shift, weights=weights):
+                    sweep(now, old, weights, first + i * shift, width)
+                    return carry
+
+                lax.fori_loop(0, sides, side, 0)
             return carry
 
-        lax.fori_loop(first_pair, last_pair, body, 0)
-
-    def inner(now, old, weights, t):
-        first = inner_first(t)
-        sweep(now, old, weights, first, cols - 2 * first)
-
-    def edges(now, old, weights, t):
-        first, width = outer_first(t), inner_first(t) - outer_first(t)
-
-        def side(i, carry):
-            sweep(now, old, weights, first + i * (cols - first - width - first), width)
-            return carry
-
-        lax.fori_loop(0, 2, side, 0)
-
-    def full(now, old, weights, t):
-        first = outer_first(t)
-        sweep(now, old, weights, first, cols - 2 * first)
-
-    both(0, pairs, inner)
+        lax.fori_loop(begin_pair, end_pair, pair, 0)
+
+    def inner(t):
+        begin = INNER + STAGE * t
+        return begin, cols - 2 * begin, 0
+
+    def edges(t):
+        begin = INNER + STAGE * t
+        width = WIDE * lax.div(begin + (steps - 1 - t) + WIDE - 1, WIDE)
+        return begin - width, width, cols - 2 * begin + width
+
+    def full(t):
+        begin = STAGE * lax.div(steps - 1 - t + STAGE - 1, STAGE)
+        return -begin, cols + 2 * begin, 0
+
+    advance(0, pairs, 1, inner)
     for f in (0, 1):
         for side in (0, 1):
             col_copy(f, side).wait()
-    both(0, pairs, edges)
-    both(pairs, steps // 2, full)
+    advance(0, pairs, 2, edges)
+    advance(pairs, steps // 2, 1, full)
 
     def store(f, q):
         src, dst = ((u_nat, uo_hbm), (v_nat, vo_hbm))[f]
@@ -193,7 +197,7 @@
             src.at[q, pl.ds(HALO, rows), :], dst.at[:, pl.ds(q * LANES, LANES)], store_sem.at[f, q])
 
     for q in range(blocks):
-        words = pl.ds(HALO + q * LANES, LANES)
+        words = pl.ds(MARGIN + q * LANES, LANES)
         for s in range(PLANES):
             lines = pl.ds(s, LANES, stride=PLANES)
             u_now = even[s + 1, words, :]
@@ -216,7 +220,7 @@
         blocks = cols // LANES
         assert rows + 2 * HALO == LANES * PLANES and steps % 2 == 0 and steps < HALO
         native = pltpu.VMEM((blocks, rows + 2 * HALO, LANES), jnp.float32)
-        level = pltpu.VMEM((PLANES + 2, cols + 2 * HALO, LANES), jnp.float32)
+        level = pltpu.VMEM((PLANES + 2, cols + 2 * MARGIN, LANES), jnp.float32)
         hbm = pl.BlockSpec(memory_space=pl.ANY)
         tile = jax.ShapeDtypeStruct((rows, cols), jnp.float32)
         dma = pltpu.SemaphoreType.DMA

time: 385 us -> 150 us (0.39)
  Pallas kernels: 377 us -> 143 us
    pallas_call x1, Pallas kernels: 377 us -> 143 us  [local_run(): pl.pallas_call(functools.partial(kernel, n_row, n_col, steps), out_shape=...]
where the time goes in v2:
time: 150 us
  Pallas kernels  143 us (95%)
  local copies, waits for them, and re-layouts  6.96 us (5%)
    pallas_call x1, Pallas kernels, local_run(): pl.pallas_call(functools.partial(kernel, n_row, n_col, steps), out_shape=...  143 us
    unnamed x4, local copies, waits for them, and re-layouts  6.96 us

profile of v2, /device:TPU:1, one launch (start us, length us, event | category | flops | bytes accessed | tf_op | source)
XLA Modules:
  0.0 150.3 jit_solution(6179886920128663610)
XLA Ops:
  0.6 142.7 %wave.1 = (f32[1024,1024]{1,0:T(8,128)}, f32[1024,1024]{1,0:T(8,128)}) custom-call(f32[1024,1024]{1,0:T(8,128)} %u_hbm.1, f32[1024,1024]{1,0:T(8,128)} %v_hbm.1, f32[3,3,48]{2,1,0:T(4,128)} %bitcast.1), custom_call_target="tpu_custom_call" | custom-call | tf_op jit(solution)/shard_map/wave/pallas_call | solution.py:227
  143.3 0.0 copy-start
  143.3 4.9 %copy.7 = f32[1024,1024]{1,0:T(8,128)} copy(f32[1024,1024]{1,0:T(8,128)} %get-tuple-element.4) | data formatting | bytes 8388608
  148.3 0.0 copy-done
  148.3 2.0 %copy.8 = f32[1024,1024]{1,0:T(8,128)} copy(f32[1024,1024]{1,0:T(8,128)S(1)} %copy-done) | data formatting | bytes 8388608
Async XLA Ops:
  143.3 5.0 %copy-start = (f32[1024,1024]{1,0:T(8,128)S(1)}, f32[1024,1024]{1,0:T(8,128)}, u32[]{:S(2)}) copy-start(f32[1024,1024]{1,0:T(8,128)} %get-tuple-element.5) | copy-start | bytes 12582916

commit v3 on v2

--- a/solution.py
+++ b/solution.py
@@ -81,7 +81,7 @@
     lax.fori_loop(0, lax.div(width, large), body, 0)
 
 
-def kernel(n_row, n_col, steps, u_hbm, v_hbm, w_ref, uo_hbm, vo_hbm, even, odd, u_nat, v_nat, load_sem, store_sem,
+def kernel(n_row, n_col, steps, u_hbm, v_hbm, w_ref, even, odd, u_nat, v_nat, load_sem,
            row_send, row_recv, col_send, col_recv):
     rows, cols = u_hbm.shape
     blocks = cols // LANES
@@ -191,6 +191,11 @@
     advance(0, pairs, 2, edges)
     advance(pairs, steps // 2, 1, full)
 
+
+def finish(even, odd, uo_hbm, vo_hbm, u_nat, v_nat, store_sem):
+    rows, cols = uo_hbm.shape
+    blocks = cols // LANES
+
     def store(f, q):
         src, dst = ((u_nat, uo_hbm), (v_nat, vo_hbm))[f]
         return pltpu.make_async_copy(
@@ -220,24 +225,32 @@
         blocks = cols // LANES
         assert rows + 2 * HALO == LANES * PLANES and steps % 2 == 0 and steps < HALO
         native = pltpu.VMEM((blocks, rows + 2 * HALO, LANES), jnp.float32)
-        level = pltpu.VMEM((PLANES + 2, cols + 2 * MARGIN, LANES), jnp.float32)
-        hbm = pl.BlockSpec(memory_space=pl.ANY)
+        level = jax.ShapeDtypeStruct((PLANES + 2, cols + 2 * MARGIN, LANES), jnp.float32)
+        hbm, vmem = pl.BlockSpec(memory_space=pltpu.HBM), pl.BlockSpec(memory_space=pltpu.VMEM)
         tile = jax.ShapeDtypeStruct((rows, cols), jnp.float32)
         dma = pltpu.SemaphoreType.DMA
-        return pl.pallas_call(
+        levels = pl.pallas_call(
             functools.partial(kernel, n_row, n_col, steps),
-            out_shape=(tile, tile),
+            out_shape=(level, level),
             in_specs=[hbm, hbm, pl.BlockSpec(memory_space=pltpu.SMEM)],
-            out_specs=(hbm, hbm),
+            out_specs=(vmem, vmem),
             scratch_shapes=[
-                level, level, native, native,
-                dma((2, blocks)), dma((2, blocks)),
+                native, native, dma((2, blocks)),
                 dma((2, 2, blocks)), dma((2, 2, blocks)), dma((2, 2)), dma((2, 2)),
             ],
             compiler_params=pltpu.CompilerParams(
-                collective_id=0, has_side_effects=True, vmem_limit_bytes=56 * 2**20),
+                collective_id=0, has_side_effects=True, vmem_limit_bytes=26 * 2**20),
             name="wave",
         )(u_tile, v_tile, jnp.transpose(stencil_w, (1, 2, 0)))
+        return pl.pallas_call(
+            finish,
+            out_shape=(tile, tile),
+            in_specs=[vmem, vmem],
+            out_specs=(hbm, hbm),
+            scratch_shapes=[native, native, dma((2, blocks))],
+            compiler_params=pltpu.CompilerParams(vmem_limit_bytes=26 * 2**20),
+            name="finish",
+        )(*levels)
 
     return jax.shard_map(
         local_run, mesh=mesh, in_specs=(tile_spec, tile_spec, P()), out_specs=(tile_spec, tile_spec), check_vma=False)

time: 150 us -> 150 us (level)
  local copies, waits for them, and re-layouts: 6.96 us -> 5.06 us
    pallas_call x0 -> x1, Pallas kernels: none -> 3.79 us  [local_run(): pl.pallas_call(finish, out_shape=(tile, tile), in_specs=[vmem, vmem], out...]
    pallas_call x1, Pallas kernels: 143 us -> 140 us  [local_run(): pl.pallas_call(functools.partial(kernel, n_row, n_col, steps), out_shape=...]
    unnamed x4 -> x6, local copies, waits for them, and re-layouts: 6.96 us -> 5.06 us
where the time goes in v3:
time: 150 us
  Pallas kernels  144 us (96%)
  local copies, waits for them, and re-layouts  5.06 us (3%)
    pallas_call x1, Pallas kernels, local_run(): pl.pallas_call(functools.partial(kernel, n_row, n_col, steps), out_shape=...  140 us
    unnamed x6, local copies, waits for them, and re-layouts  5.06 us
    pallas_call x1, Pallas kernels, local_run(): pl.pallas_call(finish, out_shape=(tile, tile), in_specs=[vmem, vmem], out...  3.79 us

profile of v3, /device:TPU:1, one launch (start us, length us, event | category | flops | bytes accessed | tf_op | source)
XLA Modules:
  0.0 149.8 jit_solution(13018437353924300956)
XLA Ops:
  0.6 0.0 copy-start
  0.6 2.2 %copy-done = f32[1024,1024]{1,0:T(8,128)S(1)} copy-done((f32[1024,1024]{1,0:T(8,128)S(1)}, f32[1024,1024]{1,0:T(8,128)}, u32[]{:S(2)}) %copy-start) | copy-done | bytes 4194328
  2.8 0.0 copy-start.1
  2.8 2.2 %copy-done.1 = f32[1024,1024]{1,0:T(8,128)S(1)} copy-done((f32[1024,1024]{1,0:T(8,128)S(1)}, f32[1024,1024]{1,0:T(8,128)}, u32[]{:S(2)}) %copy-start.1) | copy-done | bytes 4194328
  5.0 0.0 copy-start.2
  5.0 0.7 copy-done.2
  5.7 140.3 %wave.1 = (f32[11,1280,128]{2,1,0:T(8,128)S(1)}, f32[11,1280,128]{2,1,0:T(8,128)S(1)}) custom-call(f32[1024,1024]{1,0:T(8,128)S(1)} %copy-done, f32[1024,1024]{1,0:T(8,128)S(1)} %copy-done.1, f32[3,3,48]{2,1,0:T(4,128)S(1)} %bitcast.1), custom_call_target="tpu_custom_call" | custom-call | tf_op jit(solution)/shard_map/wave/pallas_call | solution.py:232
  146.0 3.8 %finish.1 = (f32[1024,1024]{1,0:T(8,128)}, f32[1024,1024]{1,0:T(8,128)}) custom-call(f32[11,1280,128]{2,1,0:T(8,128)S(1)} %get-tuple-element.4.even, f32[11,1280,128]{2,1,0:T(8,128)S(1)} %get-tuple-element.5.odd), custom_call_target="tpu_custom_call" | custom-call | tf_op jit(solution)/shard_map/finish/pallas_call | solution.py:245
Async XLA Ops:
  0.6 2.2 %copy-start = (f32[1024,1024]{1,0:T(8,128)S(1)}, f32[1024,1024]{1,0:T(8,128)}, u32[]{:S(2)}) copy-start(f32[1024,1024]{1,0:T(8,128)} %u_hbm.1) | copy-start | bytes 12582916
  2.8 2.2 %copy-start.1 = (f32[1024,1024]{1,0:T(8,128)S(1)}, f32[1024,1024]{1,0:T(8,128)}, u32[]{:S(2)}) copy-start(f32[1024,1024]{1,0:T(8,128)} %v_hbm.1) | copy-start | bytes 12582916
  5.0 0.7 copy-start.2

commit v4 on v3

--- a/solution.py
+++ b/solution.py
@@ -14,6 +14,7 @@
 INNER = 96
 STAGE = 16
 WIDE = 32
+LAST = 32
 BLOCKS = 4
 
 
@@ -27,14 +28,15 @@
     )
 
 
-def chunk(now, old, weights, start, blocks, own_ghosts):
+def chunk(now, old, weights, start, widths, left_ghosts, own_ghosts):
     centre, w00, w01, w02, w10 = weights
-
-    def taps(b, p):
-        return [now[p, pl.ds(start + (WIDE * b + d), WIDE), :] for d in (-1, 0, 1)]
-
-    def update(b, p, up, mid, down):
-        cols = pl.ds(start + WIDE * b, WIDE)
+    blocks = [(sum(widths[:i]), width) for i, width in enumerate(widths)]
+
+    def taps(block, p):
+        return [now[p, pl.ds(start + (block[0] + d), block[1]), :] for d in (-1, 0, 1)]
+
+    def update(block, p, up, mid, down):
+        cols = pl.ds(start + block[0], block[1])
         new = (
             (centre * mid[1] - old[p, cols, :])
             + w01 * (up[1] + down[1])
@@ -45,15 +47,17 @@
         old[p, cols, :] = new
         return new
 
-    cols = pl.ds(start - WIDE, WIDE)
-    ghosts = [(cols, pltpu.roll(old[PLANES, cols, :], 1, 1), pltpu.roll(old[1, cols, :], LANES - 1, 1))]
-    for b in range(blocks):
-        cols = pl.ds(start + WIDE * b, WIDE)
+    ghosts = []
+    if left_ghosts:
+        cols = pl.ds(start - WIDE, WIDE)
+        ghosts.append((cols, pltpu.roll(old[PLANES, cols, :], 1, 1), pltpu.roll(old[1, cols, :], LANES - 1, 1)))
+    for b in blocks:
+        cols = pl.ds(start + b[0], b[1])
         last = update(b, PLANES, taps(b, PLANES - 1), taps(b, PLANES), taps(b, PLANES + 1))
         first = update(b, 1, taps(b, 0), taps(b, 1), taps(b, 2))
         if own_ghosts:
             ghosts.append((cols, pltpu.roll(last, 1, 1), pltpu.roll(first, LANES - 1, 1)))
-    for b in range(blocks):
+    for b in blocks:
         up, mid = taps(b, 1), taps(b, 2)
         for p in range(2, PLANES):
             down = taps(b, p + 1)
@@ -70,18 +74,30 @@
     few = lax.div(lax.rem(width, large), small)
 
     def remainder(i, carry):
-        chunk(now, old, weights, pl.multiple_of(first + i * small, 8), 1, False)
+        chunk(now, old, weights, pl.multiple_of(first + i * small, 8), [WIDE], True, False)
         return carry
 
     def body(i, carry):
-        chunk(now, old, weights, pl.multiple_of(first + few * small + i * large, 8), BLOCKS, True)
+        chunk(now, old, weights, pl.multiple_of(first + few * small + i * large, 8), [WIDE] * BLOCKS, True, True)
         return carry
 
     lax.fori_loop(0, few, remainder, 0)
     lax.fori_loop(0, lax.div(width, large), body, 0)
 
 
-def kernel(n_row, n_col, steps, u_hbm, v_hbm, w_ref, even, odd, u_nat, v_nat, load_sem,
+def wide_sweep(now, old, weights, cols):
+    part = (cols + 2 * LAST) // 4
+    widths = [WIDE] * (part // WIDE - 1)
+    widths.append(part - sum(widths))
+
+    def body(i, carry):
+        chunk(now, old, weights, pl.multiple_of(MARGIN - LAST + i * part, 8), widths, False, True)
+        return carry
+
+    lax.fori_loop(0, 4, body, 0)
+
+
+def kernel(n_row, n_col, steps, u_hbm, v_hbm, w_hbm, even, odd, u_nat, v_nat, w_ref, load_sem, w_sem,
            row_send, row_recv, col_send, col_recv):
     rows, cols = u_hbm.shape
     blocks = cols // LANES
@@ -95,18 +111,17 @@
             src.at[:, pl.ds(q * LANES, LANES)], dst.at[q, pl.ds(HALO, rows), :], load_sem.at[f, q])
 
     def row_copy(f, side, q):
-        src, dst = ((u_hbm, u_nat), (v_hbm, v_nat))[f]
+        ref = (u_nat, v_nat)[f]
         depth = steps
-        lines = (rows - depth, 0)[side]
+        lines = (HALO + rows - depth, HALO)[side]
         place = (HALO - depth, HALO + rows)[side]
         return pltpu.make_async_remote_copy(
-            src_ref=src.at[pl.ds(lines, depth), pl.ds(q * LANES, LANES)],
-            dst_ref=dst.at[q, pl.ds(place, depth), :],
+            src_ref=ref.at[q, pl.ds(lines, depth), :], dst_ref=ref.at[q, pl.ds(place, depth), :],
             send_sem=row_send.at[f, side, q], recv_sem=row_recv.at[f, side, q],
             device_id={"row": (below, above)[side]}, device_id_type=pl.DeviceIdType.MESH)
 
     def col_copy(f, side):
-        ref, planes = ((even, pl.ds(0, PLANES + 2)), (odd, pl.ds(1, PLANES)))[f]
+        ref, planes = (even, odd)[f], pl.ds(1, PLANES)
         depth = steps
         lines = (MARGIN + cols - depth, MARGIN)[side]
         place = (MARGIN - depth, MARGIN + cols)[side]
@@ -115,6 +130,8 @@
             send_sem=col_send.at[f, side], recv_sem=col_recv.at[f, side],
             device_id={"col": (right, left)[side]}, device_id_type=pl.DeviceIdType.MESH)
 
+    load_weights = pltpu.make_async_copy(w_hbm, w_ref, w_sem)
+    load_weights.start()
     order = [0, blocks - 1] + list(range(1, blocks - 1))
     for q in order:
         for f in (0, 1):
@@ -127,6 +144,7 @@
 
     for q in order:
         for f in (0, 1):
+            load(f, q).wait()
             for side in (0, 1):
                 row_copy(f, side, q).start()
 
@@ -136,7 +154,6 @@
                 for side in (0, 1):
                     col_copy(f, side).start()
         for f in (0, 1):
-            load(f, q).wait()
             for side in (0, 1):
                 row_copy(f, side, q).wait()
 
@@ -153,43 +170,46 @@
             if s == PLANES - 1:
                 even[0, words, :] = pltpu.roll(u_now, 1, 1)
 
-    pairs = min(14, (cols - 2 * INNER - 32) // (2 * STAGE)) // 2
-
-    def advance(begin_pair, end_pair, sides, span):
+    pairs = min(8, steps // 4, (cols - 2 * INNER - 128) // (4 * STAGE))
+    assert steps - 2 * pairs <= LAST + 1
+
+    def advance(begin_pair, end_pair, step):
         def pair(v, carry):
             for odd_step, (now, old) in enumerate(((even, odd), (odd, even))):
                 t = 2 * v + odd_step
-                weights = step_weights(w_ref, t)
-                first, width, shift = span(t)
-
-                def side(i, carry, now=now, old=old, first=first, width=width, shift=shift, weights=weights):
-                    sweep(now, old, weights, first + i * shift, width)
-                    return carry
-
-                lax.fori_loop(0, sides, side, 0)
+                step(now, old, step_weights(w_ref, t), t)
             return carry
 
         lax.fori_loop(begin_pair, end_pair, pair, 0)
 
-    def inner(t):
+    def inner(now, old, weights, t):
         begin = INNER + STAGE * t
-        return begin, cols - 2 * begin, 0
-
-    def edges(t):
+        sweep(now, old, weights, begin, cols - 2 * begin)
+
+    def edges(now, old, weights, t):
         begin = INNER + STAGE * t
         width = WIDE * lax.div(begin + (steps - 1 - t) + WIDE - 1, WIDE)
-        return begin - width, width, cols - 2 * begin + width
-
-    def full(t):
-        begin = STAGE * lax.div(steps - 1 - t + STAGE - 1, STAGE)
-        return -begin, cols + 2 * begin, 0
-
-    advance(0, pairs, 1, inner)
+
+        def side(i, carry):
+            sweep(now, old, weights, begin - width + i * (cols - 2 * begin + width), width)
+            return carry
+
+        lax.fori_loop(0, 2, side, 0)
+
+    def full(now, old, weights, t):
+        wide_sweep(now, old, weights, cols)
+
+    load_weights.wait()
+    advance(0, pairs, inner)
     for f in (0, 1):
         for side in (0, 1):
             col_copy(f, side).wait()
-    advance(0, pairs, 2, edges)
-    advance(pairs, steps // 2, 1, full)
+    for place in (MARGIN - steps, MARGIN + cols):
+        words = pl.ds(place, steps)
+        even[0, words, :] = pltpu.roll(even[PLANES, words, :], 1, 1)
+        even[PLANES + 1, words, :] = pltpu.roll(even[1, words, :], LANES - 1, 1)
+    advance(0, pairs, edges)
+    advance(pairs, steps // 2, full)
 
 
 def finish(even, odd, uo_hbm, vo_hbm, u_nat, v_nat, store_sem):
@@ -232,16 +252,16 @@
         levels = pl.pallas_call(
             functools.partial(kernel, n_row, n_col, steps),
             out_shape=(level, level),
-            in_specs=[hbm, hbm, pl.BlockSpec(memory_space=pltpu.SMEM)],
+            in_specs=[hbm, hbm, hbm],
             out_specs=(vmem, vmem),
             scratch_shapes=[
-                native, native, dma((2, blocks)),
+                native, native, pltpu.SMEM((3, 3, steps), jnp.float32), dma((2, blocks)), dma(()),
                 dma((2, 2, blocks)), dma((2, 2, blocks)), dma((2, 2)), dma((2, 2)),
             ],
             compiler_params=pltpu.CompilerParams(
                 collective_id=0, has_side_effects=True, vmem_limit_bytes=26 * 2**20),
             name="wave",
-        )(u_tile, v_tile, jnp.transpose(stencil_w, (1, 2, 0)))
+        )(*(pltpu.with_memory_space_constraint(x, pltpu.HBM) for x in (u_tile, v_tile, jnp.transpose(stencil_w, (1, 2, 0)))))
         return pl.pallas_call(
             finish,
             out_shape=(tile, tile),

time: 150 us -> 141 us (0.940)
  local copies, waits for them, and re-layouts: 5.06 us -> 0 us
  Pallas kernels: 144 us -> 140 us
    unnamed x6 -> x0, local copies, waits for them, and re-layouts: 5.06 us -> none
    pallas_call x1, Pallas kernels: 140 us -> 136 us  [local_run(): pl.pallas_call(functools.partial(kernel, n_row, n_col, steps), out_shape=...]
where the time goes in v4:
time: 141 us
  Pallas kernels  140 us (99%)
    pallas_call x1, Pallas kernels, local_run(): pl.pallas_call(functools.partial(kernel, n_row, n_col, steps), out_shape=...  136 us
    pallas_call x1, Pallas kernels, local_run(): pl.pallas_call(finish, out_shape=(tile, tile), in_specs=[vmem, vmem], out...  3.79 us

profile of v4, /device:TPU:1, one launch (start us, length us, event | category | flops | bytes accessed | tf_op | source)
XLA Modules:
  0.0 140.6 jit_solution(3068283956802471936)
XLA Ops:
  0.6 136.2 %wave.1 = (f32[11,1280,128]{2,1,0:T(8,128)S(1)}, f32[11,1280,128]{2,1,0:T(8,128)S(1)}) custom-call(f32[1024,1024]{1,0:T(8,128)} %u_hbm.1, f32[1024,1024]{1,0:T(8,128)} %v_hbm.1, f32[3,3,48]{2,1,0:T(4,128)} %bitcast.1), custom_call_target="tpu_custom_call" | custom-call | tf_op jit(solution)/shard_map/wave/pallas_call | solution.py:252
  136.8 3.8 %finish.1 = (f32[1024,1024]{1,0:T(8,128)}, f32[1024,1024]{1,0:T(8,128)}) custom-call(f32[11,1280,128]{2,1,0:T(8,128)S(1)} %get-tuple-element.4.even, f32[11,1280,128]{2,1,0:T(8,128)S(1)} %get-tuple-element.5.odd), custom_call_target="tpu_custom_call" | custom-call | tf_op jit(solution)/shard_map/finish/pallas_call | solution.py:265

commit v5 on v4

--- a/solution.py
+++ b/solution.py
@@ -14,8 +14,9 @@
 INNER = 96
 STAGE = 16
 WIDE = 32
-LAST = 32
+PARTS = 2
 BLOCKS = 4
+TAPS = 5
 
 
 def step_weights(w_ref, t):
@@ -85,19 +86,19 @@
     lax.fori_loop(0, lax.div(width, large), body, 0)
 
 
-def wide_sweep(now, old, weights, cols):
-    part = (cols + 2 * LAST) // 4
+def wide_sweep(now, old, weights, cols, extra):
+    part = (cols + 2 * extra) // PARTS
     widths = [WIDE] * (part // WIDE - 1)
     widths.append(part - sum(widths))
 
     def body(i, carry):
-        chunk(now, old, weights, pl.multiple_of(MARGIN - LAST + i * part, 8), widths, False, True)
-        return carry
-
-    lax.fori_loop(0, 4, body, 0)
-
-
-def kernel(n_row, n_col, steps, u_hbm, v_hbm, w_hbm, even, odd, u_nat, v_nat, w_ref, load_sem, w_sem,
+        chunk(now, old, weights, pl.multiple_of(MARGIN - extra + i * part, 8), widths, False, True)
+        return carry
+
+    lax.fori_loop(0, PARTS, body, 0)
+
+
+def start(n_row, n_col, steps, pairs, u_hbm, v_hbm, w_hbm, even, odd, w_rows, u_nat, v_nat, w_ref, load_sem, w_sem,
            row_send, row_recv, col_send, col_recv):
     rows, cols = u_hbm.shape
     blocks = cols // LANES
@@ -147,6 +148,15 @@
             load(f, q).wait()
             for side in (0, 1):
                 row_copy(f, side, q).start()
+
+    load_weights.wait()
+
+    def spread(t, carry):
+        for k, weight in enumerate(step_weights(w_ref, t)):
+            w_rows[t, pl.ds(k, 1), :] = jnp.full((1, LANES), weight, jnp.float32)
+        return carry
+
+    lax.fori_loop(0, steps, spread, 0)
 
     for place, q in enumerate(order):
         if place == 3:
@@ -170,17 +180,14 @@
             if s == PLANES - 1:
                 even[0, words, :] = pltpu.roll(u_now, 1, 1)
 
-    pairs = min(8, steps // 4, (cols - 2 * INNER - 128) // (4 * STAGE))
-    assert steps - 2 * pairs <= LAST + 1
-
-    def advance(begin_pair, end_pair, step):
+    def advance(step):
         def pair(v, carry):
             for odd_step, (now, old) in enumerate(((even, odd), (odd, even))):
                 t = 2 * v + odd_step
                 step(now, old, step_weights(w_ref, t), t)
             return carry
 
-        lax.fori_loop(begin_pair, end_pair, pair, 0)
+        lax.fori_loop(0, pairs, pair, 0)
 
     def inner(now, old, weights, t):
         begin = INNER + STAGE * t
@@ -196,11 +203,7 @@
 
         lax.fori_loop(0, 2, side, 0)
 
-    def full(now, old, weights, t):
-        wide_sweep(now, old, weights, cols)
-
-    load_weights.wait()
-    advance(0, pairs, inner)
+    advance(inner)
     for f in (0, 1):
         for side in (0, 1):
             col_copy(f, side).wait()
@@ -208,21 +211,45 @@
         words = pl.ds(place, steps)
         even[0, words, :] = pltpu.roll(even[PLANES, words, :], 1, 1)
         even[PLANES + 1, words, :] = pltpu.roll(even[1, words, :], LANES - 1, 1)
-    advance(0, pairs, edges)
-    advance(pairs, steps // 2, full)
-
-
-def finish(even, odd, uo_hbm, vo_hbm, u_nat, v_nat, store_sem):
+    advance(edges)
+
+
+def finish(steps, begin, even_in, odd_in, w_rows, uo_hbm, vo_hbm, even, odd, u_nat, v_nat, store_sem):
+    del even_in, odd_in
     rows, cols = uo_hbm.shape
     blocks = cols // LANES
+
+    def weights_of(t):
+        return [w_rows[t, pl.ds(k, 1), :] for k in range(TAPS)]
+
+    def pair(v, carry, extra):
+        for odd_step, (now, old) in enumerate(((even, odd), (odd, even))):
+            wide_sweep(now, old, weights_of(2 * v + odd_step), cols, extra)
+        return carry
+
+    t = begin
+    while steps - t > 2:
+        extra = 8 * ((steps - 1 - t + 7) // 8)
+        until = min(steps - 2, steps - 1 - (extra - 8))
+        until += until % 2
+        until = min(until, steps - 2)
+        lax.fori_loop(t // 2, until // 2, functools.partial(pair, extra=extra), 0)
+        t = until
+    wide_sweep(even, odd, weights_of(steps - 2), cols, 8)
+
+    last = weights_of(steps - 1)
 
     def store(f, q):
         src, dst = ((u_nat, uo_hbm), (v_nat, vo_hbm))[f]
         return pltpu.make_async_copy(
-            src.at[q, pl.ds(HALO, rows), :], dst.at[:, pl.ds(q * LANES, LANES)], store_sem.at[f, q])
-
-    for q in range(blocks):
-        words = pl.ds(MARGIN + q * LANES, LANES)
+            src.at[q, pl.ds(HALO, rows), :],
+            dst.at[:, pl.ds(pl.multiple_of(q * LANES, LANES), LANES)], store_sem.at[f, q])
+
+    def step(q):
+        chunk(odd, even, last, pl.multiple_of(MARGIN + q * LANES, LANES), [WIDE] * (LANES // WIDE), False, False)
+
+    def write(q):
+        words = pl.ds(pl.multiple_of(MARGIN + q * LANES, LANES), LANES)
         for s in range(PLANES):
             lines = pl.ds(s, LANES, stride=PLANES)
             u_now = even[s + 1, words, :]
@@ -230,6 +257,15 @@
             v_nat[q, lines, :] = jnp.transpose(8.0 * (u_now - odd[s + 1, words, :]))
         for f in (0, 1):
             store(f, q).start()
+
+    def both(q, carry):
+        step(q)
+        write(q - 1)
+        return carry
+
+    step(0)
+    lax.fori_loop(1, blocks, both, 0)
+    write(blocks - 1)
     for q in range(blocks):
         for f in (0, 1):
             store(f, q).wait()
@@ -249,28 +285,31 @@
         hbm, vmem = pl.BlockSpec(memory_space=pltpu.HBM), pl.BlockSpec(memory_space=pltpu.VMEM)
         tile = jax.ShapeDtypeStruct((rows, cols), jnp.float32)
         dma = pltpu.SemaphoreType.DMA
-        levels = pl.pallas_call(
-            functools.partial(kernel, n_row, n_col, steps),
-            out_shape=(level, level),
+        pairs = min(8, steps // 4, (cols - 2 * INNER - 128) // (4 * STAGE))
+        w_rows = jax.ShapeDtypeStruct((steps, 8, LANES), jnp.float32)
+        state = pl.pallas_call(
+            functools.partial(start, n_row, n_col, steps, pairs),
+            out_shape=(level, level, w_rows),
             in_specs=[hbm, hbm, hbm],
-            out_specs=(vmem, vmem),
+            out_specs=(vmem, vmem, vmem),
             scratch_shapes=[
                 native, native, pltpu.SMEM((3, 3, steps), jnp.float32), dma((2, blocks)), dma(()),
                 dma((2, 2, blocks)), dma((2, 2, blocks)), dma((2, 2)), dma((2, 2)),
             ],
             compiler_params=pltpu.CompilerParams(
                 collective_id=0, has_side_effects=True, vmem_limit_bytes=26 * 2**20),
-            name="wave",
+            name="start",
         )(*(pltpu.with_memory_space_constraint(x, pltpu.HBM) for x in (u_tile, v_tile, jnp.transpose(stencil_w, (1, 2, 0)))))
         return pl.pallas_call(
-            finish,
-            out_shape=(tile, tile),
-            in_specs=[vmem, vmem],
-            out_specs=(hbm, hbm),
+            functools.partial(finish, steps, 2 * pairs),
+            out_shape=(tile, tile, level, level),
+            in_specs=[vmem, vmem, vmem],
+            out_specs=(hbm, hbm, vmem, vmem),
+            input_output_aliases={0: 2, 1: 3},
             scratch_shapes=[native, native, dma((2, blocks))],
             compiler_params=pltpu.CompilerParams(vmem_limit_bytes=26 * 2**20),
             name="finish",
-        )(*levels)
+        )(*state)[:2]
 
     return jax.shard_map(
         local_run, mesh=mesh, in_specs=(tile_spec, tile_spec, P()), out_specs=(tile_spec, tile_spec), check_vma=False)

time: 141 us -> 139 us (0.986)
  Pallas kernels: 140 us -> 138 us
    pallas_call x2, Pallas kernels: 140 us -> 138 us  [the longest x1 78.6 us: local_run(): pl.pallas_call(functools.partial(finish, steps, 2 * pairs), out_shape=(ti...]
where the time goes in v5:
time: 139 us
  Pallas kernels  138 us (99%)
    pallas_call x1, Pallas kernels, local_run(): pl.pallas_call(functools.partial(finish, steps, 2 * pairs), out_shape=(ti...  78.6 us
    pallas_call x1, Pallas kernels, local_run(): pl.pallas_call(functools.partial(start, n_row, n_col, steps, pairs), out_...  59.3 us

profile of v5, /device:TPU:1, one launch (start us, length us, event | category | flops | bytes accessed | tf_op | source)
XLA Modules:
  0.0 138.7 jit_solution(1138316154274240130)
XLA Ops:
  0.6 59.3 %start.1 = (f32[11,1280,128]{2,1,0:T(8,128)S(1)}, f32[11,1280,128]{2,1,0:T(8,128)S(1)}, f32[48,8,128]{2,1,0:T(8,128)S(1)}) custom-call(f32[1024,1024]{1,0:T(8,128)} %u_hbm.1, f32[1024,1024]{1,0:T(8,128)} %v_hbm.1, f32[3,3,48]{2,1,0:T(4,128)} %bitcast.1), custom_call_target="tpu_custom_call" | custom-call | tf_op jit(solution)/shard_map/start/pallas_call | solution.py:290
  60.0 78.6 %finish.1 = (f32[1024,1024]{1,0:T(8,128)}, f32[1024,1024]{1,0:T(8,128)}, f32[11,1280,128]{2,1,0:T(8,128)S(1)}, f32[11,1280,128]{2,1,0:T(8,128)S(1)}) custom-call(f32[11,1280,128]{2,1,0:T(8,128)S(1)} %get-tuple-element.7.even_in, f32[11,1280,128]{2,1,0:T(8,128)S(1)} %get-tuple-element.8.odd_in, ...), custom_call_target="tpu_custom_call", output_to_operand_aliasing={{2}: (0, {}), {3}: (1, {})} | custom-call | tf_op jit(solution)/shard_map/finish/pallas_call | solution.py:303

commit v6 on v5

--- a/solution.py
+++ b/solution.py
@@ -243,13 +243,13 @@
         src, dst = ((u_nat, uo_hbm), (v_nat, vo_hbm))[f]
         return pltpu.make_async_copy(
             src.at[q, pl.ds(HALO, rows), :],
-            dst.at[:, pl.ds(pl.multiple_of(q * LANES, LANES), LANES)], store_sem.at[f, q])
+            dst.at[:, pl.ds(q * LANES, LANES)], store_sem.at[f, q])
 
     def step(q):
-        chunk(odd, even, last, pl.multiple_of(MARGIN + q * LANES, LANES), [WIDE] * (LANES // WIDE), False, False)
+        chunk(odd, even, last, MARGIN + q * LANES, [WIDE] * (LANES // WIDE), False, False)
 
     def write(q):
-        words = pl.ds(pl.multiple_of(MARGIN + q * LANES, LANES), LANES)
+        words = pl.ds(MARGIN + q * LANES, LANES)
         for s in range(PLANES):
             lines = pl.ds(s, LANES, stride=PLANES)
             u_now = even[s + 1, words, :]
@@ -258,13 +258,10 @@
         for f in (0, 1):
             store(f, q).start()
 
-    def both(q, carry):
+    step(0)
+    for q in range(1, blocks):
         step(q)
         write(q - 1)
-        return carry
-
-    step(0)
-    lax.fori_loop(1, blocks, both, 0)
     write(blocks - 1)
     for q in range(blocks):
         for f in (0, 1):
@@ -285,7 +282,7 @@
         hbm, vmem = pl.BlockSpec(memory_space=pltpu.HBM), pl.BlockSpec(memory_space=pltpu.VMEM)
         tile = jax.ShapeDtypeStruct((rows, cols), jnp.float32)
         dma = pltpu.SemaphoreType.DMA
-        pairs = min(8, steps // 4, (cols - 2 * INNER - 128) // (4 * STAGE))
+        pairs = min(6, steps // 4, (cols - 2 * INNER - 128) // (4 * STAGE))
         w_rows = jax.ShapeDtypeStruct((steps, 8, LANES), jnp.float32)
         state = pl.pallas_call(
             functools.partial(start, n_row, n_col, steps, pairs),

time: 139 us -> 135 us (0.971)
  Pallas kernels: 138 us -> 135 us
    pallas_call x1, Pallas kernels: 59.3 us -> 48.6 us  [local_run(): pl.pallas_call(functools.partial(start, n_row, n_col, steps, pairs), out_...]
    pallas_call x1, Pallas kernels: 78.6 us -> 85.9 us  [local_run(): pl.pallas_call(functools.partial(finish, steps, 2 * pairs), out_shape=(ti...]
where the time goes in v6:
time: 135 us
  Pallas kernels  135 us (100%)
    pallas_call x1, Pallas kernels, local_run(): pl.pallas_call(functools.partial(finish, steps, 2 * pairs), out_shape=(ti...  85.9 us
    pallas_call x1, Pallas kernels, local_run(): pl.pallas_call(functools.partial(start, n_row, n_col, steps, pairs), out_...  48.6 us

profile of v6, /device:TPU:1, one launch (start us, length us, event | category | flops | bytes accessed | tf_op | source)
XLA Modules:
  0.0 135.3 jit_solution(12260238270940492213)
XLA Ops:
  0.6 48.6 %start.1 = (f32[11,1280,128]{2,1,0:T(8,128)S(1)}, f32[11,1280,128]{2,1,0:T(8,128)S(1)}, f32[48,8,128]{2,1,0:T(8,128)S(1)}) custom-call(f32[1024,1024]{1,0:T(8,128)} %u_hbm.1, f32[1024,1024]{1,0:T(8,128)} %v_hbm.1, f32[3,3,48]{2,1,0:T(4,128)} %bitcast.1), custom_call_target="tpu_custom_call" | custom-call | tf_op jit(solution)/shard_map/start/pallas_call | solution.py:287
  49.3 85.9 %finish.1 = (f32[1024,1024]{1,0:T(8,128)}, f32[1024,1024]{1,0:T(8,128)}, f32[11,1280,128]{2,1,0:T(8,128)S(1)}, f32[11,1280,128]{2,1,0:T(8,128)S(1)}) custom-call(f32[11,1280,128]{2,1,0:T(8,128)S(1)} %get-tuple-element.7.even_in, f32[11,1280,128]{2,1,0:T(8,128)S(1)} %get-tuple-element.8.odd_in, ...), custom_call_target="tpu_custom_call", output_to_operand_aliasing={{2}: (0, {}), {3}: (1, {})} | custom-call | tf_op jit(solution)/shard_map/finish/pallas_call | solution.py:300

commit v7 on v6

--- a/solution.py
+++ b/solution.py
@@ -15,7 +15,7 @@
 STAGE = 16
 WIDE = 32
 PARTS = 2
-BLOCKS = 4
+BLOCKS = (8, 4, 1)
 TAPS = 5
 
 
@@ -70,20 +70,21 @@
 
 
 def sweep(now, old, weights, first_col, width):
-    first = first_col + MARGIN
-    small, large = WIDE, WIDE * BLOCKS
-    few = lax.div(lax.rem(width, large), small)
-
-    def remainder(i, carry):
-        chunk(now, old, weights, pl.multiple_of(first + i * small, 8), [WIDE], True, False)
-        return carry
-
-    def body(i, carry):
-        chunk(now, old, weights, pl.multiple_of(first + few * small + i * large, 8), [WIDE] * BLOCKS, True, True)
-        return carry
-
-    lax.fori_loop(0, few, remainder, 0)
-    lax.fori_loop(0, lax.div(width, large), body, 0)
+    done = first_col + MARGIN
+    left = width
+    counts = []
+    for blocks in BLOCKS:
+        counts.append((blocks, lax.div(left, WIDE * blocks)))
+        left = left - counts[-1][1] * (WIDE * blocks)
+    for blocks, count in reversed(counts):
+        size = WIDE * blocks
+
+        def body(i, carry, done=done, blocks=blocks, size=size):
+            chunk(now, old, weights, pl.multiple_of(done + i * size, 8), [WIDE] * blocks, True, blocks > 1)
+            return carry
+
+        lax.fori_loop(0, count, body, 0)
+        done = done + count * size
 
 
 def wide_sweep(now, old, weights, cols, extra):
@@ -193,41 +194,45 @@
         begin = INNER + STAGE * t
         sweep(now, old, weights, begin, cols - 2 * begin)
 
-    def edges(now, old, weights, t):
-        begin = INNER + STAGE * t
-        width = WIDE * lax.div(begin + (steps - 1 - t) + WIDE - 1, WIDE)
-
-        def side(i, carry):
-            sweep(now, old, weights, begin - width + i * (cols - 2 * begin + width), width)
-            return carry
-
-        lax.fori_loop(0, 2, side, 0)
-
     advance(inner)
     for f in (0, 1):
         for side in (0, 1):
             col_copy(f, side).wait()
+
+
+def finish(steps, pairs, even_in, odd_in, w_rows, uo_hbm, vo_hbm, even, odd, u_nat, v_nat, store_sem):
+    del even_in, odd_in
+    rows, cols = uo_hbm.shape
+    blocks = cols // LANES
+
+    def weights_of(t):
+        return [w_rows[t, pl.ds(k, 1), :] for k in range(TAPS)]
+
+    def pair(v, carry, extra):
+        for odd_step, (now, old) in enumerate(((even, odd), (odd, even))):
+            wide_sweep(now, old, weights_of(2 * v + odd_step), cols, extra)
+        return carry
+
     for place in (MARGIN - steps, MARGIN + cols):
         words = pl.ds(place, steps)
         even[0, words, :] = pltpu.roll(even[PLANES, words, :], 1, 1)
         even[PLANES + 1, words, :] = pltpu.roll(even[1, words, :], LANES - 1, 1)
-    advance(edges)
-
-
-def finish(steps, begin, even_in, odd_in, w_rows, uo_hbm, vo_hbm, even, odd, u_nat, v_nat, store_sem):
-    del even_in, odd_in
-    rows, cols = uo_hbm.shape
-    blocks = cols // LANES
-
-    def weights_of(t):
-        return [w_rows[t, pl.ds(k, 1), :] for k in range(TAPS)]
-
-    def pair(v, carry, extra):
-        for odd_step, (now, old) in enumerate(((even, odd), (odd, even))):
-            wide_sweep(now, old, weights_of(2 * v + odd_step), cols, extra)
-        return carry
-
-    t = begin
+
+    for t in range(2 * pairs):
+        now, old = ((even, odd), (odd, even))[t % 2]
+        end = INNER + STAGE * t
+        width = STAGE * ((end + steps - 1 - t + STAGE - 1) // STAGE)
+        widths = [WIDE] * (width // WIDE - 1)
+        widths.append(width - sum(widths))
+
+        def side(i, carry, now=now, old=old, t=t, end=end, width=width, widths=widths):
+            left = MARGIN + end - width + i * (cols - 2 * end + width)
+            chunk(now, old, weights_of(t), pl.multiple_of(left, 8), widths, False, True)
+            return carry
+
+        lax.fori_loop(0, 2, side, 0)
+
+    t = 2 * pairs
     while steps - t > 2:
         extra = 8 * ((steps - 1 - t + 7) // 8)
         until = min(steps - 2, steps - 1 - (extra - 8))
@@ -298,7 +303,7 @@
             name="start",
         )(*(pltpu.with_memory_space_constraint(x, pltpu.HBM) for x in (u_tile, v_tile, jnp.transpose(stencil_w, (1, 2, 0)))))
         return pl.pallas_call(
-            functools.partial(finish, steps, 2 * pairs),
+            functools.partial(finish, steps, pairs),
             out_shape=(tile, tile, level, level),
             in_specs=[vmem, vmem, vmem],
             out_specs=(hbm, hbm, vmem, vmem),

time: 135 us -> 134 us (level)
  Pallas kernels: 135 us -> 133 us
    pallas_call x1, Pallas kernels: 48.6 us -> 34.6 us  [local_run(): pl.pallas_call(functools.partial(start, n_row, n_col, steps, pairs), out_...]
    pallas_call x1, Pallas kernels: 85.9 us -> 98.5 us  [local_run(): pl.pallas_call(functools.partial(finish, steps, pairs), out_shape=(tile,...]
where the time goes in v7:
time: 134 us
  Pallas kernels  133 us (99%)
    pallas_call x1, Pallas kernels, local_run(): pl.pallas_call(functools.partial(finish, steps, pairs), out_shape=(tile,...  98.5 us
    pallas_call x1, Pallas kernels, local_run(): pl.pallas_call(functools.partial(start, n_row, n_col, steps, pairs), out_...  34.6 us

profile of v7, /device:TPU:1, one launch (start us, length us, event | category | flops | bytes accessed | tf_op | source)
XLA Modules:
  0.0 134.0 jit_solution(1706791754075666251)
XLA Ops:
  0.6 34.6 %start.1 = (f32[11,1280,128]{2,1,0:T(8,128)S(1)}, f32[11,1280,128]{2,1,0:T(8,128)S(1)}, f32[48,8,128]{2,1,0:T(8,128)S(1)}) custom-call(f32[1024,1024]{1,0:T(8,128)} %u_hbm.1, f32[1024,1024]{1,0:T(8,128)} %v_hbm.1, f32[3,3,48]{2,1,0:T(4,128)} %bitcast.1), custom_call_target="tpu_custom_call" | custom-call | tf_op jit(solution)/shard_map/start/pallas_call | solution.py:292
  35.2 98.5 %finish.1 = (f32[1024,1024]{1,0:T(8,128)}, f32[1024,1024]{1,0:T(8,128)}, f32[11,1280,128]{2,1,0:T(8,128)S(1)}, f32[11,1280,128]{2,1,0:T(8,128)S(1)}) custom-call(f32[11,1280,128]{2,1,0:T(8,128)S(1)} %get-tuple-element.7.even_in, f32[11,1280,128]{2,1,0:T(8,128)S(1)} %get-tuple-element.8.odd_in, ...), custom_call_target="tpu_custom_call", output_to_operand_aliasing={{2}: (0, {}), {3}: (1, {})} | custom-call | tf_op jit(solution)/shard_map/finish/pallas_call | solution.py:305

commit v8 on v7

--- a/solution.py
+++ b/solution.py
@@ -159,20 +159,17 @@
 
     lax.fori_loop(0, steps, spread, 0)
 
-    for place, q in enumerate(order):
-        if place == 3:
-            for f in (0, 1):
-                for side in (0, 1):
-                    col_copy(f, side).start()
+    def take_rows(q):
         for f in (0, 1):
             for side in (0, 1):
                 row_copy(f, side, q).wait()
 
+    def lay_out(q):
+        words = pl.ds(pl.multiple_of(MARGIN + q * LANES, LANES), LANES)
         for s in range(PLANES):
             lines = pl.ds(s, LANES, stride=PLANES)
             u_now = 0.25 * u_nat[q, lines, :]
             u_old = u_now - 0.125 * v_nat[q, lines, :]
-            words = pl.ds(MARGIN + q * LANES, LANES)
             u_now = jnp.transpose(u_now)
             even[s + 1, words, :] = u_now
             odd[s + 1, words, :] = jnp.transpose(u_old)
@@ -181,6 +178,31 @@
             if s == PLANES - 1:
                 even[0, words, :] = pltpu.roll(u_now, 1, 1)
 
+    def first_step(q, widths):
+        begin = pl.multiple_of(MARGIN + INNER + (q - 1) * LANES, 8)
+        chunk(even, odd, step_weights(w_ref, 0), begin, widths, False, True)
+
+    take_rows(0)
+    lay_out(0)
+    take_rows(blocks - 1)
+    for f in (0, 1):
+        col_copy(f, 1).start()
+    lay_out(blocks - 1)
+    take_rows(1)
+    for f in (0, 1):
+        col_copy(f, 0).start()
+    lay_out(1)
+    first_step(1, [WIDE] * (LANES // WIDE))
+
+    def next_block(q, carry):
+        take_rows(q)
+        lay_out(q)
+        first_step(q, [WIDE] * (LANES // WIDE))
+        return carry
+
+    lax.fori_loop(2, blocks - 1, next_block, 0)
+    first_step(blocks - 1, [WIDE] * ((2 * LANES - 2 * INNER) // WIDE))
+
     def advance(step):
         def pair(v, carry):
             for odd_step, (now, old) in enumerate(((even, odd), (odd, even))):
@@ -192,7 +214,7 @@
 
     def inner(now, old, weights, t):
         begin = INNER + STAGE * t
-        sweep(now, old, weights, begin, cols - 2 * begin)
+        sweep(now, old, weights, begin, jnp.where(t == 0, 0, cols - 2 * begin))
 
     advance(inner)
     for f in (0, 1):
@@ -287,7 +309,7 @@
         hbm, vmem = pl.BlockSpec(memory_space=pltpu.HBM), pl.BlockSpec(memory_space=pltpu.VMEM)
         tile = jax.ShapeDtypeStruct((rows, cols), jnp.float32)
         dma = pltpu.SemaphoreType.DMA
-        pairs = min(6, steps // 4, (cols - 2 * INNER - 128) // (4 * STAGE))
+        pairs = min(7, steps // 4, (cols - 2 * INNER - 128) // (4 * STAGE))
         w_rows = jax.ShapeDtypeStruct((steps, 8, LANES), jnp.float32)
         state = pl.pallas_call(
             functools.partial(start, n_row, n_col, steps, pairs),

time: 134 us -> 134 us (level)
    pallas_call x1, Pallas kernels: 34.6 us -> 36.7 us  [local_run(): pl.pallas_call(functools.partial(start, n_row, n_col, steps, pairs), out_...]
    pallas_call x1, Pallas kernels: 98.5 us -> 96.8 us  [local_run(): pl.pallas_call(functools.partial(finish, steps, pairs), out_shape=(tile,...]
where the time goes in v8:
time: 134 us
  Pallas kernels  133 us (99%)
    pallas_call x1, Pallas kernels, local_run(): pl.pallas_call(functools.partial(finish, steps, pairs), out_shape=(tile,...  96.8 us
    pallas_call x1, Pallas kernels, local_run(): pl.pallas_call(functools.partial(start, n_row, n_col, steps, pairs), out_...  36.7 us

profile of v8, /device:TPU:1, one launch (start us, length us, event | category | flops | bytes accessed | tf_op | source)
XLA Modules:
  0.0 134.2 jit_solution(4511461207342532985)
XLA Ops:
  0.6 36.7 %start.1 = (f32[11,1280,128]{2,1,0:T(8,128)S(1)}, f32[11,1280,128]{2,1,0:T(8,128)S(1)}, f32[48,8,128]{2,1,0:T(8,128)S(1)}) custom-call(f32[1024,1024]{1,0:T(8,128)} %u_hbm.1, f32[1024,1024]{1,0:T(8,128)} %v_hbm.1, f32[3,3,48]{2,1,0:T(4,128)} %bitcast.1), custom_call_target="tpu_custom_call" | custom-call | tf_op jit(solution)/shard_map/start/pallas_call | solution.py:314
  37.3 96.8 %finish.1 = (f32[1024,1024]{1,0:T(8,128)}, f32[1024,1024]{1,0:T(8,128)}, f32[11,1280,128]{2,1,0:T(8,128)S(1)}, f32[11,1280,128]{2,1,0:T(8,128)S(1)}) custom-call(f32[11,1280,128]{2,1,0:T(8,128)S(1)} %get-tuple-element.7.even_in, f32[11,1280,128]{2,1,0:T(8,128)S(1)} %get-tuple-element.8.odd_in, ...), custom_call_target="tpu_custom_call", output_to_operand_aliasing={{2}: (0, {}), {3}: (1, {})} | custom-call | tf_op jit(solution)/shard_map/finish/pallas_call | solution.py:327

commit v9 on v8

--- a/solution.py
+++ b/solution.py
@@ -192,15 +192,19 @@
     for f in (0, 1):
         col_copy(f, 0).start()
     lay_out(1)
-    first_step(1, [WIDE] * (LANES // WIDE))
+
+    def ready_step(q, carry):
+        first_step(q, [WIDE] * (LANES // WIDE))
+        return carry
 
     def next_block(q, carry):
+        lax.fori_loop(q - 1, q, ready_step, 0)
         take_rows(q)
         lay_out(q)
-        first_step(q, [WIDE] * (LANES // WIDE))
         return carry
 
     lax.fori_loop(2, blocks - 1, next_block, 0)
+    first_step(blocks - 2, [WIDE] * (LANES // WIDE))
     first_step(blocks - 1, [WIDE] * ((2 * LANES - 2 * INNER) // WIDE))
 
     def advance(step):

time: 134 us -> 133 us (level)
  no operation moved by 1% of the time
where the time goes in v9:
time: 133 us
  Pallas kernels  132 us (99%)
    pallas_call x1, Pallas kernels, local_run(): pl.pallas_call(functools.partial(finish, steps, pairs), out_shape=(tile,...  96.8 us
    pallas_call x1, Pallas kernels, local_run(): pl.pallas_call(functools.partial(start, n_row, n_col, steps, pairs), out_...  35.6 us

profile of v9, /device:TPU:1, one launch (start us, length us, event | category | flops | bytes accessed | tf_op | source)
XLA Modules:
  0.0 133.2 jit_solution(2773191298728715087)
XLA Ops:
  0.6 35.6 %start.1 = (f32[11,1280,128]{2,1,0:T(8,128)S(1)}, f32[11,1280,128]{2,1,0:T(8,128)S(1)}, f32[48,8,128]{2,1,0:T(8,128)S(1)}) custom-call(f32[1024,1024]{1,0:T(8,128)} %u_hbm.1, f32[1024,1024]{1,0:T(8,128)} %v_hbm.1, f32[3,3,48]{2,1,0:T(4,128)} %bitcast.1), custom_call_target="tpu_custom_call" | custom-call | tf_op jit(solution)/shard_map/start/pallas_call | solution.py:318
  36.2 96.8 %finish.1 = (f32[1024,1024]{1,0:T(8,128)}, f32[1024,1024]{1,0:T(8,128)}, f32[11,1280,128]{2,1,0:T(8,128)S(1)}, f32[11,1280,128]{2,1,0:T(8,128)S(1)}) custom-call(f32[11,1280,128]{2,1,0:T(8,128)S(1)} %get-tuple-element.7.even_in, f32[11,1280,128]{2,1,0:T(8,128)S(1)} %get-tuple-element.8.odd_in, ...), custom_call_target="tpu_custom_call", output_to_operand_aliasing={{2}: (0, {}), {3}: (1, {})} | custom-call | tf_op jit(solution)/shard_map/finish/pallas_call | solution.py:331

commit v10 on v9

--- a/solution.py
+++ b/solution.py
@@ -313,7 +313,7 @@
         hbm, vmem = pl.BlockSpec(memory_space=pltpu.HBM), pl.BlockSpec(memory_space=pltpu.VMEM)
         tile = jax.ShapeDtypeStruct((rows, cols), jnp.float32)
         dma = pltpu.SemaphoreType.DMA
-        pairs = min(7, steps // 4, (cols - 2 * INNER - 128) // (4 * STAGE))
+        pairs = min(8, steps // 4, (cols - 2 * INNER - 128) // (4 * STAGE))
         w_rows = jax.ShapeDtypeStruct((steps, 8, LANES), jnp.float32)
         state = pl.pallas_call(
             functools.partial(start, n_row, n_col, steps, pairs),

time: 133 us -> 133 us (level)
    pallas_call x1, Pallas kernels: 35.6 us -> 37.3 us  [local_run(): pl.pallas_call(functools.partial(start, n_row, n_col, steps, pairs), out_...]
    pallas_call x1, Pallas kernels: 96.8 us -> 95.2 us  [local_run(): pl.pallas_call(functools.partial(finish, steps, pairs), out_shape=(tile,...]
where the time goes in v10:
time: 133 us
  Pallas kernels  133 us (100%)
    pallas_call x1, Pallas kernels, local_run(): pl.pallas_call(functools.partial(finish, steps, pairs), out_shape=(tile,...  95.2 us
    pallas_call x1, Pallas kernels, local_run(): pl.pallas_call(functools.partial(start, n_row, n_col, steps, pairs), out_...  37.3 us

profile of v10, /device:TPU:1, one launch (start us, length us, event | category | flops | bytes accessed | tf_op | source)
XLA Modules:
  0.0 133.4 jit_solution(16258502408389525808)
XLA Ops:
  0.6 37.3 %start.1 = (f32[11,1280,128]{2,1,0:T(8,128)S(1)}, f32[11,1280,128]{2,1,0:T(8,128)S(1)}, f32[48,8,128]{2,1,0:T(8,128)S(1)}) custom-call(f32[1024,1024]{1,0:T(8,128)} %u_hbm.1, f32[1024,1024]{1,0:T(8,128)} %v_hbm.1, f32[3,3,48]{2,1,0:T(4,128)} %bitcast.1), custom_call_target="tpu_custom_call" | custom-call | tf_op jit(solution)/shard_map/start/pallas_call | solution.py:318
  38.0 95.2 %finish.1 = (f32[1024,1024]{1,0:T(8,128)}, f32[1024,1024]{1,0:T(8,128)}, f32[11,1280,128]{2,1,0:T(8,128)S(1)}, f32[11,1280,128]{2,1,0:T(8,128)S(1)}) custom-call(f32[11,1280,128]{2,1,0:T(8,128)S(1)} %get-tuple-element.7.even_in, f32[11,1280,128]{2,1,0:T(8,128)S(1)} %get-tuple-element.8.odd_in, ...), custom_call_target="tpu_custom_call", output_to_operand_aliasing={{2}: (0, {}), {3}: (1, {})} | custom-call | tf_op jit(solution)/shard_map/finish/pallas_call | solution.py:331

commit v11 on v9

--- a/solution.py
+++ b/solution.py
@@ -182,6 +182,10 @@
         begin = pl.multiple_of(MARGIN + INNER + (q - 1) * LANES, 8)
         chunk(even, odd, step_weights(w_ref, 0), begin, widths, False, True)
 
+    def second_step(q, widths):
+        begin = pl.multiple_of(MARGIN + INNER + STAGE + (q - 1) * LANES, 8)
+        chunk(odd, even, step_weights(w_ref, 1), begin, widths, False, True)
+
     take_rows(0)
     lay_out(0)
     take_rows(blocks - 1)
@@ -197,8 +201,13 @@
         first_step(q, [WIDE] * (LANES // WIDE))
         return carry
 
+    def ready_second(q, carry):
+        second_step(q, [WIDE] * (LANES // WIDE))
+        return carry
+
     def next_block(q, carry):
         lax.fori_loop(q - 1, q, ready_step, 0)
+        lax.fori_loop(jnp.where(q == 2, 1, q - 2), q - 1, ready_second, 0)
         take_rows(q)
         lay_out(q)
         return carry
@@ -206,6 +215,8 @@
     lax.fori_loop(2, blocks - 1, next_block, 0)
     first_step(blocks - 2, [WIDE] * (LANES // WIDE))
     first_step(blocks - 1, [WIDE] * ((2 * LANES - 2 * INNER) // WIDE))
+    lax.fori_loop(blocks - 3, blocks - 1, ready_second, 0)
+    second_step(blocks - 1, [2 * LANES - 2 * INNER - 2 * STAGE])
 
     def advance(step):
         def pair(v, carry):
@@ -218,7 +229,7 @@
 
     def inner(now, old, weights, t):
         begin = INNER + STAGE * t
-        sweep(now, old, weights, begin, jnp.where(t == 0, 0, cols - 2 * begin))
+        sweep(now, old, weights, begin, jnp.where(t < 2, 0, cols - 2 * begin))
 
     advance(inner)
     for f in (0, 1):

time: 133 us -> 133 us (level)
  no operation moved by 1% of the time
where the time goes in v11:
time: 133 us
  Pallas kernels  132 us (99%)
    pallas_call x1, Pallas kernels, local_run(): pl.pallas_call(functools.partial(finish, steps, pairs), out_shape=(tile,...  96.8 us
    pallas_call x1, Pallas kernels, local_run(): pl.pallas_call(functools.partial(start, n_row, n_col, steps, pairs), out_...  35.1 us

profile of v11, /device:TPU:1, one launch (start us, length us, event | category | flops | bytes accessed | tf_op | source)
XLA Modules:
  0.0 132.7 jit_solution(10886103028793119809)
XLA Ops:
  0.6 35.1 %start.1 = (f32[11,1280,128]{2,1,0:T(8,128)S(1)}, f32[11,1280,128]{2,1,0:T(8,128)S(1)}, f32[48,8,128]{2,1,0:T(8,128)S(1)}) custom-call(f32[1024,1024]{1,0:T(8,128)} %u_hbm.1, f32[1024,1024]{1,0:T(8,128)} %v_hbm.1, f32[3,3,48]{2,1,0:T(4,128)} %bitcast.1), custom_call_target="tpu_custom_call" | custom-call | tf_op jit(solution)/shard_map/start/pallas_call | solution.py:329
  35.7 96.8 %finish.1 = (f32[1024,1024]{1,0:T(8,128)}, f32[1024,1024]{1,0:T(8,128)}, f32[11,1280,128]{2,1,0:T(8,128)S(1)}, f32[11,1280,128]{2,1,0:T(8,128)S(1)}) custom-call(f32[11,1280,128]{2,1,0:T(8,128)S(1)} %get-tuple-element.7.even_in, f32[11,1280,128]{2,1,0:T(8,128)S(1)} %get-tuple-element.8.odd_in, ...), custom_call_target="tpu_custom_call", output_to_operand_aliasing={{2}: (0, {}), {3}: (1, {})} | custom-call | tf_op jit(solution)/shard_map/finish/pallas_call | solution.py:342

commit v12 on v11

--- a/solution.py
+++ b/solution.py
@@ -324,7 +324,7 @@
         hbm, vmem = pl.BlockSpec(memory_space=pltpu.HBM), pl.BlockSpec(memory_space=pltpu.VMEM)
         tile = jax.ShapeDtypeStruct((rows, cols), jnp.float32)
         dma = pltpu.SemaphoreType.DMA
-        pairs = min(7, steps // 4, (cols - 2 * INNER - 128) // (4 * STAGE))
+        pairs = min(8, steps // 4, (cols - 2 * INNER - 128) // (4 * STAGE))
         w_rows = jax.ShapeDtypeStruct((steps, 8, LANES), jnp.float32)
         state = pl.pallas_call(
             functools.partial(start, n_row, n_col, steps, pairs),

time: 133 us -> 133 us (level)
    pallas_call x1, Pallas kernels: 35.1 us -> 36.8 us  [local_run(): pl.pallas_call(functools.partial(start, n_row, n_col, steps, pairs), out_...]
    pallas_call x1, Pallas kernels: 96.8 us -> 95.2 us  [local_run(): pl.pallas_call(functools.partial(finish, steps, pairs), out_shape=(tile,...]
where the time goes in v12:
time: 133 us
  Pallas kernels  132 us (99%)
    pallas_call x1, Pallas kernels, local_run(): pl.pallas_call(functools.partial(finish, steps, pairs), out_shape=(tile,...  95.2 us
    pallas_call x1, Pallas kernels, local_run(): pl.pallas_call(functools.partial(start, n_row, n_col, steps, pairs), out_...  36.8 us

profile of v12, /device:TPU:1, one launch (start us, length us, event | category | flops | bytes accessed | tf_op | source)
XLA Modules:
  0.0 132.8 jit_solution(15168201846837130856)
XLA Ops:
  0.6 36.8 %start.1 = (f32[11,1280,128]{2,1,0:T(8,128)S(1)}, f32[11,1280,128]{2,1,0:T(8,128)S(1)}, f32[48,8,128]{2,1,0:T(8,128)S(1)}) custom-call(f32[1024,1024]{1,0:T(8,128)} %u_hbm.1, f32[1024,1024]{1,0:T(8,128)} %v_hbm.1, f32[3,3,48]{2,1,0:T(4,128)} %bitcast.1), custom_call_target="tpu_custom_call" | custom-call | tf_op jit(solution)/shard_map/start/pallas_call | solution.py:329
  37.4 95.2 %finish.1 = (f32[1024,1024]{1,0:T(8,128)}, f32[1024,1024]{1,0:T(8,128)}, f32[11,1280,128]{2,1,0:T(8,128)S(1)}, f32[11,1280,128]{2,1,0:T(8,128)S(1)}) custom-call(f32[11,1280,128]{2,1,0:T(8,128)S(1)} %get-tuple-element.7.even_in, f32[11,1280,128]{2,1,0:T(8,128)S(1)} %get-tuple-element.8.odd_in, ...), custom_call_target="tpu_custom_call", output_to_operand_aliasing={{2}: (0, {}), {3}: (1, {})} | custom-call | tf_op jit(solution)/shard_map/finish/pallas_call | solution.py:342
